TPU v7x, 128 devices: a whole 4x4x4 slice. The times are simulated.
128 devices in a mesh: tp: 2 (over core), fsdp: 64 (over z, y, x).
Axes of the slice: x: 4, y: 4, z: 4, core: 2. Of those that a mesh axis runs over, the one named last changes fastest.
Arguments:
- x: bfloat16 [128, 1024, 1024], P('fsdp')
- grad_y: bfloat16 [128, 1024, 1024], P('fsdp')
- w_qkv: bfloat16 [1024, 3, 16, 64], P('fsdp', None, 'tp')
- w_out: bfloat16 [16, 64, 1024], P('tp', None, 'fsdp')
- w_ff: bfloat16 [1024, 2, 2816], P('fsdp', None, 'tp')
- w_down: bfloat16 [2816, 1024], P('tp', 'fsdp')
Outputs:
- output 1: bfloat16 [128, 1024, 1024], P('fsdp')
- output 2: bfloat16 [128, 1024, 1024], P('fsdp')
- output 3: float32 [1024, 3, 16, 64], P('fsdp', None, 'tp')
- output 4: float32 [16, 64, 1024], P('tp', None, 'fsdp')
- output 5: float32 [1024, 2, 2816], P('fsdp', None, 'tp')
- output 6: float32 [2816, 1024], P('tp', 'fsdp')
All inputs are finite; a program needn't handle non-finite values.
Results may differ from a plain program's by a relative error of at most 0.0160394.
Values are sent between devices in bfloat16 or wider.
A program may use at most 1 GiB of HBM per device.

v0:
```python
import functools

import jax
import jax.numpy as jnp
import numpy as np
from jax import lax
from jax.experimental import pallas as pl
from jax.experimental.pallas import tpu as pltpu
from jax.sharding import PartitionSpec as P

MESH_ID = pl.DeviceIdType.MESH
SIDE = 4
PIECE = 16
ORDERS = ((2, 1, 0), (1, 0, 2), (0, 2, 1))
BOTH = ((0, 1), (1, -1))
PHASES = THREE = range(3)
TWO = range(2)


class Torus:
    def __init__(self):
        self.core = lax.axis_index('tp')
        self.index = lax.axis_index('fsdp')
        plane, x = lax.div(self.index, SIDE), lax.rem(self.index, SIDE)
        self.at = (lax.div(plane, SIDE), lax.rem(plane, SIDE), x)
        self.partner = (1 - self.core, self.index)
        self.moved = {(axis, by): lax.rem(at + (by + SIDE), SIDE) for axis, at in enumerate(self.at) for by in range(-2, 3)}
        self.peers = {(axis, by): self.place(axis, self.moved[axis, by]) for axis in THREE for by in (-1, 1, 2)}

    def place(self, axis, coord):
        pos = list(self.at)
        pos[axis] = coord
        z, y, x = pos
        return (self.core, (z * SIDE + y) * SIDE + x)

    def shift(self, axis, by):
        return self.moved[axis, by]

    def peer(self, axis, by):
        return self.peers[axis, by]

    def neighbours(self, reach=1):
        return [device for (_, by), device in self.peers.items() if by <= reach]

    def tell(self, sem, devices):
        for device in devices:
            pl.semaphore_signal(sem, inc=1, device_id=device, device_id_type=MESH_ID)

    def barrier(self, devices):
        sem = pltpu.get_barrier_semaphore()
        self.tell(sem, devices)
        pl.semaphore_wait(sem, len(devices))


def pair_of(sems, *at):
    return sems.at[(0,) + at], sems.at[(1,) + at]


def in_order(*calls):
    def run():
        for call in calls:
            call()
    return run


def span(cols):
    (off, width), *rest = cols
    return pl.ds(off, width + sum(w for _, w in rest))


class Gather:
    SEMS = 7

    def __init__(self, net, shard, out, cols, shift, sems, first, direct=False):
        self.net, self.shard, self.out, self.cols, self.moved, self.sems, self.first, self.direct = net, shard, out, cols, shift, sems, first, direct

    def block(self, colour, phase, coord, half=None):
        order = ORDERS[colour]
        off, width = self.cols[colour]
        pick = list(self.net.at)
        for axis in order[:phase]:
            pick[axis] = pl.ds(0, SIDE)
        pick[order[phase]] = coord
        if half is not None and phase:
            pick[order[0]] = pl.ds(half * 2, 2)
        elif half is not None:
            cut = width - width // 256 * 128
            off, width = (off + cut, width - cut) if half else (off, cut)
        return self.out.at[(*pick, slice(None), pl.ds(off, width))] if width else None

    def copy(self, phase, colour, relay, d, by):
        axis = ORDERS[colour][phase]
        far = relay and self.direct
        if far and d:
            return None
        by = 2 if far else by
        back = -by if relay and not far else 0
        dst = src = self.block(colour, phase, self.net.shift(axis, back), d if relay and not far else None)
        if dst is None:
            return None
        if not phase and (far or not relay):
            off, width = self.cols[colour]
            src = self.shard.at[:, pl.ds(off + self.moved, width)]
        return pltpu.make_async_remote_copy(src, dst, *self.sem(phase, relay), device_id=self.net.peer(axis, by), device_id_type=MESH_ID)

    def sem(self, phase, relay):
        return pair_of(self.sems, self.first + 2 * phase + relay)

    def each(self, phase, relay):
        for d, by in BOTH:
            for colour in THREE:
                desc = self.copy(phase, colour, relay, d, by)
                if desc is not None:
                    desc.start()

    def wait(self, phase, relay, side):
        pick = [pl.ds(0, SIDE)] * phase + [pl.ds(0, 2 - relay)] + [0, 0]
        ref = self.out.at[tuple(reversed(pick[:3])) + (slice(None), span(self.cols))]
        pltpu.make_async_copy(ref, ref, self.sem(phase, relay)[side]).wait()

    def own(self):
        at = self.net.at
        cols = span(self.cols)
        src = self.shard.at[:, pl.ds(cols.start + self.moved, cols.size)]
        return pltpu.make_async_copy(src, self.out.at[(*at, slice(None), cols)], self.sems.at[0, self.first + self.SEMS - 1])

    def arrive(self, phase):
        if self.direct:
            self.wait(phase, 0, 1)
        self.wait(phase, 1, 1)

    def start(self, phase):
        if phase:
            self.arrive(phase - 1)
        if phase == 1:
            self.own().wait()
        for relay in range(1 + self.direct):
            self.each(phase, relay)
        if not phase:
            self.own().start()

    def relay(self, phase):
        self.wait(phase, 0, 1)
        self.each(phase, 1)

    def finish(self):
        self.arrive(PHASES[-1])
        for phase in PHASES:
            for relay in TWO:
                self.wait(phase, relay, 0)

    def stages(self):
        steps = (self.start,) if self.direct else (self.start, self.relay)
        return [functools.partial(f, p) for p in PHASES for f in steps] + [self.finish]


class Scatter:
    SEMS = 9

    def __init__(self, net, part, cols, bufs, sems, first):
        self.net, self.part, self.cols, self.bufs, self.sems, self.first = net, part, cols, bufs, sems, first

    @staticmethod
    def scratch(cols):
        shapes = []
        for _, w in cols:
            shapes += [(3, 2, 2, SIDE, PIECE, w), (3, 2, 2, PIECE, w), (3, 2, PIECE // 2, w)]
        return [pltpu.VMEM(s, jnp.float32) for s in shapes]

    def buf(self, colour, phase):
        return self.bufs[colour * len(PHASES) + phase]

    def block(self, colour, phase, coord, half):
        order = ORDERS[colour]
        off, width = self.cols[colour]
        pick = [pl.ds(0, SIDE)] * 3
        for axis in order[:phase]:
            pick[axis] = self.net.at[axis]
        pick[order[phase]] = coord
        rows = pl.ds(0, PIECE)
        rest = sorted(order[phase + 1:])
        if rest:
            pick[rest[0]] = pl.ds(2 * half, 2)
        else:
            rows = pl.ds(PIECE // 2 * half, PIECE // 2)
        return self.part.at[(*pick, rows, pl.ds(off, width))]

    def copy(self, phase, colour, kind, d, by):
        axis = ORDERS[colour][phase]
        buf = self.buf(colour, phase)
        if kind == 2:
            src = buf.at[0, d]
        elif kind:
            src = self.block(colour, phase, self.net.shift(axis, by), 1 - d)
        else:
            src = self.block(colour, phase, self.net.shift(axis, 2), d)
        return pltpu.make_async_remote_copy(src, buf.at[kind, d], *self.sem(phase, kind), device_id=self.net.peer(axis, by), device_id_type=MESH_ID)

    def sem(self, phase, kind):
        return pair_of(self.sems, self.first + len(PHASES) * phase + kind)

    def wait(self, phase, kind, side):
        pick = [0] * (phase + 1) + [pl.ds(0, SIDE)] * (2 - phase)
        ref = self.part.at[tuple(pick) + (slice(None), span(self.cols))]
        pltpu.make_async_copy(ref, ref, self.sem(phase, kind)[side]).wait()

    def start(self, phase, kind):
        for d, by in BOTH:
            for colour in THREE:
                self.copy(phase, colour, kind, d, by).start()

    def relay(self, phase):
        self.wait(phase, 0, 1)
        for colour in THREE:
            buf = self.buf(colour, phase)
            for d, by in BOTH:
                buf[0, d] = buf[0, d] + self.block(colour, phase, self.net.shift(ORDERS[colour][phase], by), d)[...]
        self.start(phase, 2)

    def merge(self, phase):
        for kind in (1, 2):
            self.wait(phase, kind, 1)
        for colour in THREE:
            buf = self.buf(colour, phase)
            for half in TWO:
                mine = self.block(colour, phase, self.net.at[ORDERS[colour][phase]], half)
                mine[...] = mine[...] + buf[1, 1 - half] + buf[2, half]
        if phase + 1 < len(PHASES):
            for kind in TWO:
                self.start(phase + 1, kind)

    def finish(self):
        for phase in PHASES:
            for kind in PHASES:
                self.wait(phase, kind, 0)

    def stages(self):
        calls = [functools.partial(self.start, 0, kind) for kind in TWO]
        for phase in PHASES:
            calls += [functools.partial(self.relay, phase), functools.partial(self.merge, phase)]
        return calls[:-1] + [in_order(calls[-1], self.finish)]

    def result(self):
        return self.part[self.net.at]


def cut_three(width, off=0, turn=0):
    tiles = width // 128
    sizes = [(tiles + (2 + turn - i) % 3) // 3 * 128 for i in THREE]
    return [(off + sum(sizes[:i]), s) for i, s in enumerate(sizes)]


def plan(text, *sets):
    left = [iter(s) for s in sets]
    return [(hook, next(left[int(which)])) for hook, field in enumerate(text.split(',')) for which in field]


def halves_of(calls, first=0):
    return [[((when - first) // 2, call) for when, call in calls if when >= first and (when - first) % 2 == odd] for odd in TWO]


def run_at(hook, calls):
    for when, call in calls:
        pl.when(hook == when)(call)


F32, BF16 = jnp.float32, jnp.bfloat16
QB = 256
LANES = 128
HALF = LANES // 2
CLIP = 8.0
MIB = 2**20


def nt(a, b):
    return lax.dot_general(a, b, (((1,), (1,)), ((), ())), preferred_element_type=F32)


def nn(a, b):
    return jnp.dot(a, b, preferred_element_type=F32)


def tn(a, b):
    return lax.dot_general(a, b, (((0,), (0,)), ((), ())), preferred_element_type=F32)


def along(reduce, values):
    return reduce(values, axis=-1, keepdims=True)


def head_masks(paired):
    lane = lax.broadcasted_iota(jnp.int32, (1, LANES), 1)
    first = lane % HALF < HALF // 2 if paired else lane < HALF
    return first, jnp.logical_not(first)


def causal_tile(key_axis):
    dims = (QB, 2 * QB) if key_axis == 0 else (2 * QB, QB)
    return lax.broadcasted_iota(jnp.int32, dims, key_axis) <= lax.broadcasted_iota(jnp.int32, dims, 1 - key_axis) % QB


def by_head(values, masks):
    return jnp.concatenate([jnp.where(m, values, jnp.zeros((), BF16)) for m in masks], axis=0)


def attend_pair(q_ref, k_ref, v_ref, o_ref, lse_ref):
    masks = head_masks(True)
    key, val = k_ref[...], v_ref[...]
    causal = causal_tile(1)
    first = head_masks(False)[0]
    for lo in reversed(strips(q_ref.shape[0], QB)):
        hi = lo + QB
        query = by_head(q_ref[lo:hi, :], masks)
        diag = jnp.where(causal, nt(query, key[lo:hi]), -1e30)
        top = along(jnp.max, diag)
        if lo:
            past = nt(query, key[:lo])
            top = jnp.maximum(top, along(jnp.max, past))
            past = jnp.exp(past - top)
        diag = jnp.exp(diag - top)
        total = along(jnp.sum, diag)
        if lo:
            total = total + along(jnp.sum, past)
        scale = 1.0 / total
        acc = nn((diag * scale).astype(BF16), val[lo:hi])
        if lo:
            acc = acc + nn((past * scale).astype(BF16), val[:lo])
        o_ref[lo:hi, :] = jnp.where(first, acc[:QB], acc[QB:]).astype(BF16)
        lse = jnp.broadcast_to(top + jnp.log(total), acc.shape).T
        for h in TWO:
            lse_ref[h:h + 1, lo:hi] = lse[:1, h * QB:(h + 1) * QB]


def attend_pair_back(q_ref, k_ref, v_ref, do_ref, lse_ref, dk_ref, dv_ref, put_dq):
    seq = q_ref.shape[0]
    qmask, vmask = head_masks(True), head_masks(False)
    key, val = k_ref[...], v_ref[...]
    key_t = key.astype(F32).T.astype(BF16)
    causal = causal_tile(0)
    first = lax.broadcasted_iota(jnp.int32, (LANES, 1), 0) % HALF < HALF // 2

    def products(lo):
        hi = lo + QB
        query, dout = by_head(q_ref[lo:hi, :], qmask), by_head(do_ref[lo:hi, :], vmask)
        return query, dout, nt(key[:hi], query), nt(val[:hi], dout)

    ahead = products(seq - QB)
    for lo in reversed(strips(seq, QB)):
        hi = lo + QB
        query, dout, score, grad = ahead
        if lo:
            ahead = products(lo - QB)
        prob = jnp.exp(score - jnp.concatenate([lse_ref[h:h + 1, lo:hi] for h in TWO], axis=1))
        diag = jnp.where(causal, prob[lo:], 0.0)
        prob = jnp.concatenate([prob[:lo], diag], axis=0) if lo else diag
        ds = (prob * (grad - jnp.sum(prob * grad, axis=0, keepdims=True))).astype(BF16)
        both = nn(key_t[:, :hi], ds)
        put_dq(lo, hi, jnp.where(first, both[:, :QB], both[:, QB:]).T)
        dv, dk = nn(prob.astype(BF16), dout), nn(ds, query)
        if hi == seq:
            dv_ref[...] = dv
            dk_ref[...] = dk
        else:
            dv_ref[:hi, :] += dv
            dk_ref[:hi, :] += dk


def swap_halves(values):
    return pltpu.roll(values, HALF, axis=1)


COARSE = 32


def tables(seq, head):
    freq = 10000.0 ** (-np.arange(0, head, 2, dtype=np.float64) / head)
    angles = [np.tile(np.arange(seq // COARSE)[:, None] * step * freq, LANES // len(freq)) for step in (1, COARSE)]
    return np.stack([np.stack([np.cos(angle), np.sin(angle)]) for angle in angles]).astype(np.float32)


def spread_tables(table_ref, cos_ref, sin_ref):
    fine_cos, fine_sin = table_ref[0]
    sign = jnp.where(lax.broadcasted_iota(jnp.int32, (1, LANES), 1) < HALF, -1.0, 1.0)

    def body(i):
        rows = aligned(i * COARSE, COARSE)
        cos, sin = table_ref[1, :, pl.ds(i, 1), :]
        cos_ref[rows, :] = fine_cos * cos - fine_sin * sin
        sin_ref[rows, :] = (fine_sin * cos + fine_cos * sin) * sign

    repeat(cos_ref.shape[0] // COARSE, body)


def repeat(count, body):
    def step(i, carry):
        body(i)
        return carry

    lax.fori_loop(0, count, step, 0)


def side_by_side(halves, j):
    return jnp.concatenate([halves[2 * j], halves[2 * j + 1]], axis=1)


def aligned(at, size):
    return pl.ds(pl.multiple_of(at, size), size)


def norm_rows(values):
    mean = along(jnp.mean, values)
    centered = values - mean
    inv = lax.rsqrt(along(jnp.mean, centered * centered) + 1e-5)
    return centered * inv, inv


def norm_grad(grad, normed, inv):
    mean = along(jnp.mean, grad)
    proj = along(jnp.mean, grad * normed)
    return inv * (grad - mean - normed * proj)


def params(collective_id, limit=63):
    return pltpu.CompilerParams(collective_id=collective_id, has_side_effects=True, vmem_limit_bytes=limit * MIB)


def grid_step():
    return pl.program_id(0), pl.num_programs(0) - 1


def dma(*shape):
    return pltpu.SemaphoreType.DMA(shape)


def shape(dtype, *dims):
    return jax.ShapeDtypeStruct(dims, dtype)


HBM = pl.BlockSpec(memory_space=pltpu.HBM)
WHOLE = pl.BlockSpec(memory_space=pltpu.VMEM)


def lanes(part):
    return slice(LANES * part, LANES * (part + 1))


def strips(width, size):
    return range(0, width, size)


def rows_of(size, width, index):
    return pl.BlockSpec((size, width), lambda step: (index(step), 0))


def fixed(block, index=(0, 0)):
    return pl.BlockSpec(block, lambda *grid: index, pipeline_mode=pl.Buffered(buffer_count=1))


def project_pair(n1_ref, weight, cos_ref, sin_ref, qkv_ref, keep_ref):
    for lo in strips(n1_ref.shape[0], QB):
        rows = slice(lo, lo + QB)
        raw = nn(n1_ref[rows, :], weight)
        keep_ref[rows, :] = (jnp.abs(raw) < CLIP).astype(F32).astype(BF16)
        raw = jnp.clip(raw, -CLIP, CLIP)
        for part in THREE:
            cols = lanes(part)
            tile = raw[:, cols]
            if part < 2:
                tile = tile * cos_ref[rows, :] + swap_halves(tile) * sin_ref[rows, :]
            if not part:
                tile = tile * 0.125
            qkv_ref[rows, cols] = tile.astype(BF16)


def swap_middle(tile):
    quarter = lax.broadcasted_iota(jnp.int32, tile.shape, 1) // (LANES // 4)
    up, down = pltpu.roll(tile, LANES // 4, axis=1), pltpu.roll(tile, LANES - LANES // 4, axis=1)
    return jnp.where(quarter == 1, down, jnp.where(quarter == 2, up, tile))


CHUNK = 256
CHUNK_STEPS = 4
FRONT_PLAN = '014560145260124530,4,245,,13,,345,,2,,4,,3,,5,,,5'
SCATTER_PLAN = '00,,,,,11,,,20,,,,12,,,20,1,,20,12,10,2,102,,102'
LAST_PLAN = '00,,1,202,,31,3,,413,442,31,04,231,402,13,402,,1,403201342'


def to_partner(net, src, dst, send, recv):
    return pltpu.make_async_remote_copy(src, dst, send, recv, device_id=net.partner, device_id_type=MESH_ID)


def front_kernel(x_hbm, qkv_shard, out_shard, ff_shard, down_shard, table_ref, qkv_ref, keep_ref, o_ref, lse_ref, h_hbm, n1_hbm, wq_hbm, wo_hbm, wf_hbm,
                 x_all, n1, w, shards, o_all, part, got, h_buf, wo, sems, gather_sems, load_sem, h_sem, cos_ref, sin_ref, o_buf):
    step, last = grid_step()
    turn = step - 1
    batch, pairs, seq = o_all.shape[:3]
    b, p = turn % batch, turn // batch
    half = CHUNK // 2
    chunks = seq // CHUNK
    ff = down_shard.shape[1]
    net = Torus()
    width = 3 * LANES
    heads_end, out_end = width * pairs, (width + LANES) * pairs
    places = [(w, cut_three(width, width * j), 0) for j in range(pairs)] + [
              (wo_hbm, cut_three(LANES * pairs), heads_end), (wf_hbm, cut_three(3 * ff), out_end)]
    gathers = [Gather(net, shards, out, cols, shift, gather_sems, i * Gather.SEMS, i < pairs) for i, (out, cols, shift) in enumerate(places)]
    strip = x_all.shape[0] // CHUNK_STEPS

    def rows_at(i):
        return aligned(i * strip, strip)

    def load(i):
        return pltpu.make_async_copy(x_hbm.at[rows_at(i)], x_all.at[rows_at(i)], load_sem.at[i])

    def save(i):
        return pltpu.make_async_copy(n1.at[rows_at(i)], n1_hbm.at[rows_at(i)], load_sem.at[i])

    save_weight = pltpu.make_async_copy(w, wq_hbm, load_sem.at[CHUNK_STEPS])

    def normalize(i):
        load(i).wait()
        n1[rows_at(i), :] = norm_rows(x_all[rows_at(i), :].astype(F32))[0].astype(BF16)
        save(i).start()

    def normalize_half(first):
        repeat(CHUNK_STEPS // 2, lambda i: normalize(first + i))

    spread = functools.partial(spread_tables, table_ref, cos_ref, sin_ref)
    calls = plan(FRONT_PLAN, *([*g.stages()] for g in gathers), [in_order(spread, functools.partial(normalize_half, 0)), functools.partial(normalize_half, CHUNK_STEPS // 2)])

    @pl.when(step == 0)
    def _():
        for i in range(CHUNK_STEPS):
            load(i).start()
        for i in THREE:
            heads = qkv_shard[:, i].astype(F32).swapaxes(0, 1)
            for j in range(pairs):
                tile = side_by_side(heads, j)
                shards[:, lanes(3 * j + i)] = (swap_middle(tile) if i < 2 else tile).astype(BF16)
        for j in range(pairs):
            shards[:, lanes(3 * pairs + j)] = side_by_side(out_shard, j)
        both = ff_shard[...].astype(F32)
        for i in range(ff // LANES):
            for j in TWO:
                shards[:, lanes(4 * pairs + 2 * i + j)] = both[:, j, lanes(i)].astype(BF16)
        shards[:, out_end + 2 * ff:] = down_shard[...]
        net.barrier(net.neighbours(2) + [net.partner])
        for when, call in calls:
            if not when:
                call()

    begin, end = halves_of(calls, 1)
    run_at(turn, begin)

    @pl.when(turn >= 0)
    def _():
        weight = w[:, :, :, :, pl.ds(pl.multiple_of(width * p, LANES), width)].reshape(n1.shape[1], width)
        project_pair(n1.at[aligned(b * seq, seq)], weight, cos_ref, sin_ref, qkv_ref, keep_ref)
        q_ref, k_ref, v_ref = (qkv_ref.at[:, pl.ds(LANES * i, LANES)] for i in THREE)
        attend_pair(q_ref, k_ref, v_ref, o_ref, lse_ref.at[0, 0])
        o_all[b, p] = o_ref[...]

    run_at(turn, end)

    def rows_in(c, core):
        return aligned(c * CHUNK + core * half, half)

    def part_copy(b, c):
        return to_partner(net, part.at[b, rows_in(c, 1 - net.core)], got.at[b, c], *pair_of(sems, 0, b, c))

    def rows_out(b, c, core):
        return aligned(b * seq + c * CHUNK + core * half, half)

    def h_copy(b, c, core):
        return to_partner(net, h_buf.at[b, c], h_hbm.at[rows_out(b, c, core)], *pair_of(sems, 1, b, c))

    def h_local(b, c):
        return pltpu.make_async_copy(h_buf.at[b, c], h_hbm.at[rows_out(b, c, net.core)], h_sem.at[b, c])

    def project(b):
        o_buf[...] = jnp.concatenate([o_all[b, j] for j in range(pairs)], axis=1)
        weight = wo[...].reshape(part.shape[2], LANES * pairs)

        def body(c):
            rows = aligned(c * CHUNK, CHUNK)
            part[b, rows, :] = nt(o_buf[rows, :], weight)
            part_copy(b, c).start()

        repeat(chunks, body)

    def combine(b):
        def body(c):
            part_copy(b, c).wait()
            own = rows_in(c, net.core)
            h_buf[b, c] = (x_all[rows_out(b, c, net.core), :].astype(F32) + (part[b, own, :] + got[b, c])).astype(BF16)
            h_copy(b, c, net.core).start()
            h_local(b, c).start()

        repeat(chunks, body)

    def settle():
        for b in range(batch):
            for c in range(chunks):
                h_copy(b, c, net.core).wait_send()
                h_local(b, c).wait()
                h_copy(b, c, 1 - net.core).wait_recv()
        for i in range(CHUNK_STEPS):
            save(i).wait()
        save_weight.wait()

    fetch = pltpu.make_async_copy(wo_hbm, wo, h_sem.at[0, 0])
    run_at(last - step, [(2, fetch.start), (2, save_weight.start), (1, fetch.wait), (0, functools.partial(combine, 0))])

    @pl.when(step + 1 >= last)
    def _():
        project(step + 1 - last)

    run_at(last - step, [(0, functools.partial(combine, 1)), (0, settle)])
    run_at(turn + 1, begin[-1:])


def front(x, qkv_shard, out_shard, ff_shard, down_shard, table, batch, seq, collective_id):
    pairs = len(out_shard) // 2
    rows, d = x.shape
    width = 3 * LANES
    chunks = seq // CHUNK
    vm = pltpu.VMEM
    torus = (SIDE, SIDE, SIDE, PIECE)
    shards = [s.size // PIECE for s in (qkv_shard, out_shard, ff_shard, down_shard)]
    turn = lambda s: jnp.maximum(s - 1, 0)
    head = lambda width: pl.BlockSpec((seq, width), lambda s: (turn(s) % batch, turn(s) // batch))
    return pl.pallas_call(
        front_kernel,
        grid=(1 + batch * pairs,),
        in_specs=[HBM] + [WHOLE] * 5,
        out_specs=[head(width), head(width), head(LANES), pl.BlockSpec((1, 1, 2, seq), lambda s: (turn(s) % batch, turn(s) // batch, 0, 0))] + [HBM] * 5,
        out_shape=[shape(BF16, rows, width * pairs)] * 2 + [shape(BF16, rows, LANES * pairs), shape(F32, batch, pairs, 2, seq), shape(BF16, rows, d), shape(BF16, rows, d),
                   shape(BF16, *torus, shards[0]), shape(BF16, *torus, shards[1]), shape(BF16, *torus, shards[2] + shards[3])],
        scratch_shapes=[vm((rows, d), BF16), vm((rows, d), BF16), vm(torus + (width * pairs,), BF16), vm((PIECE, sum(shards)), BF16),
                        vm((batch, pairs, seq, LANES), BF16), vm((batch, seq, d), F32), vm((batch, chunks, CHUNK // 2, d), F32), vm((batch, chunks, CHUNK // 2, d), BF16),
                        vm(torus + (shards[1],), BF16), dma(2, 2, batch, chunks), dma(2, (pairs + 2) * Gather.SEMS), dma(CHUNK_STEPS + 1), dma(batch, chunks)] + [vm((seq, LANES), F32)] * 2 + [vm((seq, LANES * pairs), BF16)],
        compiler_params=params(collective_id),
        name='front',
    )(x, qkv_shard, out_shard, ff_shard, down_shard, table)


class Exchange:
    def __init__(self, net, rows, partials, results, sems, local_sem):
        self.net, self.rows, self.partials, self.results, self.sems, self.local_sem = net, rows, partials, results, sems, local_sem

    def half(self, core, at=0):
        return aligned(at * self.rows + core * (self.rows // 2), self.rows // 2)

    def part(self, which, at):
        part, got = self.partials[which]
        return to_partner(self.net, part.at[at % 2, self.half(1 - self.net.core)], got.at[at], *pair_of(self.sems, which, at))

    def total(self, which, at):
        part, got = self.partials[which]
        self.part(which, at).wait()
        return part[at % 2, self.half(self.net.core), :] + got[at]

    def results_of(self, at, core, act):
        for i, (buf, hbm) in enumerate(self.results):
            act(buf.at[at % 2], hbm.at[self.half(core, at)], pair_of(self.sems, len(self.partials) + i, at), self.local_sem.at[i, at % 2])

    def publish(self, at):
        def act(buf, rows, sem, local_sem):
            to_partner(self.net, buf, rows, *sem).start()
            pltpu.make_async_copy(buf, rows, local_sem).start()
        self.results_of(at, self.net.core, act)

    def settle(self, at):
        def act(buf, rows, sem, local_sem):
            to_partner(self.net, buf, rows, *sem).wait_send()
            pltpu.make_async_copy(buf, rows, local_sem).wait()
        self.results_of(at, self.net.core, act)
        self.results_of(at, 1 - self.net.core, lambda buf, rows, sem, local_sem: to_partner(self.net, buf, rows, *sem).wait_recv())


def mlp_kernel(blocks, h_ref, gy_ref, wff_ref, wd_ref, y_hbm, gh_hbm, gh32_ref, acts_hbm, n2_ref, gd_hbm,
               saved, grad_down, part_y, part_g, got_y, got_g, y_buf, gh_buf, h_own, gy_own, sems, local_sem, save_sem):
    step, final = grid_step()
    rows, d = h_ref.shape
    ff = wd_ref.shape[1]
    acts = saved.at[step % 2]
    gug, act = acts.at[:, pl.ds(0, 2 * ff)], acts.at[:, pl.ds(2 * ff, ff)]

    def save(at):
        return pltpu.make_async_copy(saved.at[at % 2], acts_hbm.at[aligned(at * rows, rows)], save_sem.at[at % 2])

    save_grad = pltpu.make_async_copy(grad_down, gd_hbm, save_sem.at[2])
    net = Torus()
    swap = Exchange(net, rows, ((part_y, got_y), (part_g, got_g)), ((y_buf, y_hbm), (gh_buf, gh_hbm)), sems, local_sem)

    @pl.when(step == 0)
    def _():
        net.barrier([net.partner])

    @pl.when((step > 1) & (step < blocks))
    def _():
        save(step - 2).wait()

    @pl.when(step < blocks)
    def _():
        n2, _ = norm_rows(h_ref[...].astype(F32))
        n2 = n2.astype(BF16)
        n2_ref[...] = n2
        gy = gy_ref[...]
        for j in strips(ff, QB):
            w = min(QB, ff - j)
            gact = nn(gy, wd_ref[:, j:j + w])
            for i in range(j, j + w, LANES):
                at, mid, end = 2 * i, 2 * i + LANES, 2 * i + QB
                ug = nn(n2, wff_ref[:, at:end])
                up, gate = ug[:, :LANES], ug[:, LANES:]
                sig = 1.0 / (1.0 + jnp.exp(-gate))
                silu = gate * sig
                act[:, i:i + LANES] = (silu * up).astype(BF16)
                ga = gact[:, i - j:i - j + LANES]
                gug[:, at:mid] = (ga * silu).astype(BF16)
                gug[:, mid:end] = (ga * up * sig * (1.0 + gate * (1.0 - sig))).astype(BF16)

        for which, left, right, part in ((0, act, wd_ref, part_y), (1, gug, wff_ref, part_g)):
            for j in strips(d, QB):
                part[step % 2, :, j:j + QB] = nt(left[...], right[j:j + QB, :])
            swap.part(which, step).start()
        save(step).start()
        accumulate(grad_down, step == 0, gy, act)

    @pl.when(step == blocks - 1)
    def _():
        save_grad.start()

    @pl.when(step > 2)
    def _():
        swap.settle(step - 3)

    @pl.when(step > 0)
    def _():
        done = step - 1
        hidden = h_own[...].astype(F32)
        normed, inv = norm_rows(hidden)
        y_buf[done % 2] = (hidden + swap.total(0, done)).astype(BF16)
        gh = gy_own[...].astype(F32) + norm_grad(swap.total(1, done), normed, inv)
        gh32_ref[...] = gh
        gh_buf[done % 2] = gh.astype(BF16)
        swap.publish(done)

    own = swap.half(net.core)
    h_own[...] = h_ref[own, :]
    gy_own[...] = gy_ref[own, :]

    @pl.when(step == blocks)
    def _():
        for at in (blocks - 2, blocks - 1):
            swap.settle(at)
            save(at).wait()
        save_grad.wait()


def mlp(h, gy, weights, collective_id, block=512):
    rows, d = h.shape
    ff = weights.shape[1] // 3
    half = block // 2
    blocks = rows // block
    torus = (SIDE, SIDE, SIDE, PIECE)
    row = lambda width: rows_of(block, width, lambda i: jnp.minimum(i, blocks - 1))
    vm = pltpu.VMEM
    return pl.pallas_call(
        functools.partial(mlp_kernel, blocks),
        grid=(blocks + 1,),
        in_specs=[row(d), row(d), fixed((d, 2 * ff)), fixed((d, ff), (0, 2))],
        out_specs=[HBM, HBM, rows_of(half, d, lambda i: jnp.maximum(i - 1, 0)), HBM, row(d), HBM],
        out_shape=[shape(BF16, rows, d), shape(BF16, rows, d), shape(F32, rows // 2, d), shape(BF16, rows, 3 * ff), shape(BF16, rows, d), shape(F32, *torus, ff)],
        scratch_shapes=[vm((2, block, 3 * ff), BF16), vm(torus + (ff,), F32)] + [vm((2, block, d), F32)] * 2 + [vm((blocks, half, d), F32)] * 2 + [vm((2, half, d), BF16)] * 2 + [vm((half, d), BF16)] * 2 + [dma(2, 4, blocks), dma(2, 2), dma(3)],
        compiler_params=params(collective_id),
        name='mlp',
    )(h, gy, weights, weights)


def accumulate(part, first, left, right):
    for j in strips(right.shape[1], QB):
        w = min(QB, right.shape[1] - j)
        prod = tn(left, right[:, j:j + w]).reshape(part.shape[:-1] + (w,))
        at = slice(j, j + w)
        part[..., at] = jnp.where(first, 0.0, part[..., at]) + prod


SETS = 3
HEAD_STEP = (SETS - 1) * CHUNK_STEPS


def back_kernel(pairs, gd_hbm, n2_ref, act_ref, qkv_ref, lse_ref, gh_ref, wo_ref, o_ref, keep_ref, table_ref,
                g_ref, gw_ref, gd_ref, gff_ref, cos_ref, sin_ref, do_ref, dk_ref, dv_ref, parts, sems, load_sem, *bufs):
    step, final = grid_step()
    turn = step - HEAD_STEP
    p = turn % pairs
    half = gh_ref.shape[0] // 2
    net = Torus()
    per = len(bufs) // SETS
    scatters = [Scatter(net, parts.at[i], cut_three(parts.shape[-1], turn=i), bufs[per * i:per * i + per], sems, i * Scatter.SEMS) for i in range(SETS)]
    calls = plan(SCATTER_PLAN, *(s.stages() for s in scatters))
    begin, end = halves_of(calls, HEAD_STEP + 1)

    @pl.when(step == 0)
    def _():
        load = pltpu.make_async_copy(gd_hbm, parts.at[0], load_sem.at[0])
        load.start()
        spread_tables(table_ref, cos_ref, sin_ref)
        net.barrier(net.neighbours())
        load.wait()
        for when, call in calls:
            if not when:
                call()

    @pl.when(turn < 0)
    def _():
        accumulate(parts.at[1 + step // CHUNK_STEPS], step % CHUNK_STEPS == 0, n2_ref[...], act_ref)

    run_at(step + 1, [c for c in calls if 0 < c[0] <= HEAD_STEP])

    def put(part, lo, hi, values):
        cols = lanes(part)
        if part < 2:
            values = values * cos_ref[lo:hi, :] - swap_halves(values) * sin_ref[lo:hi, :]
        g_ref[lo:hi, cols] = (values * keep_ref[lo:hi, cols].astype(F32)).astype(BF16)

    def put_dq(lo, hi, dq):
        put(0, lo, hi, dq * 0.125)

    @pl.when(turn >= 0)
    def _():
        @pl.when(p == 0)
        def _():
            gw_ref[...] = jnp.where(turn == 0, 0.0, gw_ref[...])

            def body(i):
                rows = aligned(i * half, half)
                gh = gh_ref[rows, :]
                dout = nn(gh, wo_ref[...]).astype(BF16)
                for j in range(pairs):
                    do_ref[j, rows, :] = dout[:, lanes(j)]
                gw_ref[...] += tn(gh, o_ref[rows, :])

            repeat(len(TWO), body)

        run_at(turn, begin)
        q_ref, k_ref, v_ref = (qkv_ref.at[:, pl.ds(LANES * i, LANES)] for i in THREE)
        attend_pair_back(q_ref, k_ref, v_ref, do_ref.at[p], lse_ref.at[0, 0], dk_ref, dv_ref, put_dq)
        seq = q_ref.shape[0]
        put(1, 0, seq, dk_ref[...])
        put(2, 0, seq, dv_ref[...])
        run_at(turn, end)

    @pl.when(step == final)
    def _():
        gd_ref[...], *halves = [s.result() for s in scatters]
        tiles = jnp.concatenate(halves, axis=1)
        for i in strips(tiles.shape[1], LANES):
            at = i // QB * LANES
            gff_ref[:, i // LANES % 2, at:at + LANES] = tiles[:, i:i + LANES]


def back(gd, n2, acts, qkv, lse, gh, wo_t, o, keep, table, batch, seq, pairs, collective_id):
    rows, d = n2.shape
    ff = acts.shape[1] // SETS
    block = rows // CHUNK_STEPS
    turn = lambda s: jnp.maximum(s - HEAD_STEP, 0)
    head = pl.BlockSpec((seq, 3 * LANES), lambda s: (turn(s) // pairs, turn(s) % pairs))
    late = lambda s: jnp.where(s < HEAD_STEP, s % CHUNK_STEPS, CHUNK_STEPS - 1)
    vm = pltpu.VMEM
    per_seq = lambda width: rows_of(seq, width, lambda s: turn(s) // pairs)
    return pl.pallas_call(
        functools.partial(back_kernel, pairs),
        grid=(HEAD_STEP + batch * pairs,),
        in_specs=[HBM, rows_of(block, d, late), pl.BlockSpec((block, ff), lambda s: (late(s), jnp.minimum(s // CHUNK_STEPS, 1))), head, pl.BlockSpec((1, 1, 2, seq), lambda s: (turn(s) // pairs, turn(s) % pairs, 0, 0)),
                  per_seq(d), fixed(wo_t.shape), per_seq(LANES * pairs), head, WHOLE],
        out_specs=[head, fixed(wo_t.shape), WHOLE, WHOLE],
        out_shape=[shape(BF16, *qkv.shape), shape(F32, *wo_t.shape), shape(F32, PIECE, ff), shape(F32, PIECE, 2, ff)],
        scratch_shapes=[vm((seq, LANES), F32)] * 2 + [vm((pairs, seq, LANES), BF16)] + [vm((seq, LANES), F32)] * 2 + [vm((SETS, SIDE, SIDE, SIDE, PIECE, ff), F32),
                        dma(2, SETS * Scatter.SEMS), dma(1)] + [s for i in range(SETS) for s in Scatter.scratch(cut_three(ff, turn=i))],
        compiler_params=params(collective_id),
        name='back',
    )(gd, n2, acts, qkv, lse, gh, wo_t, o, keep, table)


def last_kernel(pairs, blocks, n1_ref, g_ref, x_ref, g_row, gh_ref, w_ref, gout_hbm, gx_hbm, gout_ref, gw_ref,
                part_out, part_qkv, part, got, buf, sems, scatter_sems, local_sem, *bufs):
    step, final = grid_step()
    turn = step - pairs
    rows, d = x_ref.shape
    net = Torus()
    per = len(bufs) // (pairs + 1)
    parts = [part_out] + [part_qkv.at[j] for j in range(pairs)]
    scatters = [Scatter(net, s, cut_three(s.shape[-1], turn=i), bufs[per * i:per * i + per], scatter_sems, i * Scatter.SEMS) for i, s in enumerate(parts)]
    calls = plan(LAST_PLAN, *(s.stages() for s in scatters))
    swap = Exchange(net, rows, ((part, got),), ((buf, gx_hbm),), sems, local_sem)

    @pl.when(step == 0)
    def _():
        load = pltpu.make_async_copy(gout_hbm, part_out, local_sem.at[1, 0])
        load.start()
        net.barrier(net.neighbours() + [net.partner])
        load.wait()

    begin, end = halves_of(calls)
    run_at(step, begin)

    @pl.when(turn < 0)
    def _():
        size = n1_ref.shape[0] // len(TWO)

        def body(i):
            accumulate(part_qkv.at[step], i == 0, n1_ref[aligned(i * size, size), :], g_ref.at[aligned(i * size, size)])

        repeat(len(TWO), body)

    @pl.when((turn >= 0) & (turn < blocks))
    def _():
        for j in strips(d, QB):
            part[turn % 2, :, j:j + QB] = nt(g_row[...], w_ref[j:j + QB, :])
        swap.part(0, turn).start()

    run_at(step, end)

    @pl.when(turn > 2)
    def _():
        swap.settle(turn - 3)

    @pl.when(turn > 0)
    def _():
        done = turn - 1
        normed, inv = norm_rows(x_ref[swap.half(net.core), :].astype(F32))
        buf[done % 2] = (gh_ref[...] + norm_grad(swap.total(0, done), normed, inv)).astype(BF16)
        swap.publish(done)

    @pl.when(turn == blocks)
    def _():
        for when, call in calls:
            if when > 2 * (pairs + blocks) + 1:
                call()
        for at in (blocks - 2, blocks - 1):
            swap.settle(at)
        out, *sums = [s.result() for s in scatters]
        halves = slice(HALF), slice(HALF, LANES)
        for j in range(pairs):
            for h, cols in enumerate(halves):
                gout_ref[2 * j + h] = out[:, lanes(j)][:, cols]
        for i in THREE:
            tiles = [swap_middle(s[:, lanes(i)]) if i < 2 else s[:, lanes(i)] for s in sums]
            gw_ref[:, i] = jnp.stack([t[:, cols] for t in tiles for cols in halves]).swapaxes(0, 1)


def last(x, n1, g, gh32, w, gout, pairs, collective_id, block=512):
    rows, d = x.shape
    blocks = rows // block
    late = lambda n, width, by: rows_of(n, width, lambda s: jnp.clip(s - pairs - by, 0, blocks - 1))
    head = pl.BlockSpec((rows, 3 * LANES), lambda s: (0, jnp.minimum(s, pairs - 1)))
    vm = pltpu.VMEM
    half = block // 2
    torus = (SIDE, SIDE, SIDE, PIECE)
    gout = gout.reshape(torus + (-1,))
    return pl.pallas_call(
        functools.partial(last_kernel, pairs, blocks),
        grid=(pairs + blocks + 1,),
        in_specs=[fixed((rows, d)), head, late(block, d, 1), late(block, g.shape[1], 0), late(half, d, 1), fixed(w.shape), HBM],
        out_specs=[HBM, WHOLE, WHOLE],
        out_shape=[shape(BF16, rows, d), shape(F32, 2 * pairs, PIECE, HALF), shape(F32, PIECE, 3, 2 * pairs, HALF)],
        scratch_shapes=[vm(gout.shape, F32), vm((pairs,) + torus + (3 * LANES,), F32), vm((2, block, d), F32), vm((blocks, half, d), F32), vm((2, half, d), BF16),
                        dma(2, 2, blocks), dma(2, (pairs + 1) * Scatter.SEMS), dma(2, 2)] + Scatter.scratch(cut_three(gout.shape[-1])) + Scatter.scratch(cut_three(3 * LANES)) * pairs,
        compiler_params=params(collective_id, 46),
        name='last',
    )(n1, g, x, g, gh32, w, gout)


def device_step(x, grad_y, w_qkv, w_out, w_ff, w_down):
    batch, seq, d = x.shape
    heads, head = w_qkv.shape[2:]
    pairs = heads // 2
    table = jnp.asarray(tables(seq, head))
    ids = iter(range(4))
    x2, gy = (v.reshape(batch * seq, d) for v in (x, grad_y))
    qkv, keep, o, lse, h, n1, *weights = front(x2, w_qkv, w_out.swapaxes(1, 2), w_ff, w_down.T, table, batch, seq, next(ids))
    wq, wo_t, wf = (w.reshape(d, w.shape[-1]) for w in weights)
    y, gh, gh32, acts, n2, gd = mlp(h, gy, wf, next(ids))
    g, gout, gd, gff = back(gd, n2, acts, qkv, lse, gh, wo_t, o, keep, table, batch, seq, pairs, next(ids))
    gx, gout, gqkv = last(x2, n1, g, gh32, wq, gout, pairs, next(ids))
    return y.reshape(x.shape), gx.reshape(x.shape), gqkv, gout.swapaxes(1, 2), gff, gd.T


def solution(mesh):
    specs = (P('fsdp'), P('fsdp'), P('fsdp', None, 'tp'), P('tp', None, 'fsdp'), P('fsdp', None, 'tp'), P('tp', 'fsdp'))
    return jax.shard_map(device_step, mesh=mesh, in_specs=specs, out_specs=specs, check_vma=False)
```

profile of v0, /device:TPU:1, one launch (start us, length us, event | category | flops | bytes accessed | tf_op | source)
XLA Modules:
  0.0 277.4 jit_solution(2580155764699597034)
XLA Ops:
  0.6 73.8 %front.1 = (bf16[2048,1536]{1,0:T(8,128)(2,1)}, bf16[2048,1536]{1,0:T(8,128)(2,1)}, bf16[2048,512]{1,0:T(8,128)(2,1)}, f32[2,4,2,1024]{3,2,1,0:T(2,128)}, bf16[2...) custom-call(bf16[2048,1024]{1,0:T(8,128)(2,1)} %bitcast.17, ...), custom_call_target="tpu_custom_call" | custom-call | tf_op jit(solution)/shard_map/front/pallas_call | solution.py:632
  74.4 62.4 %mlp.1 = (bf16[2048,1024]{1,0:T(8,128)(2,1)}, bf16[2048,1024]{1,0:T(8,128)(2,1)}, f32[1024,1024]{1,0:T(8,128)}, bf16[2048,4224]{1,0:T(8,128)(2,1)}, bf16[2048,10...) custom-call(bf16[2048,1024]{1,0:T(8,128)(2,1)} %get-tuple-element.28.h_ref, bf16[2048,1024]{1,0:T(8,128)(2,1)} %bitcast.19, ...), custom_call_target="tpu_custom_call" | custom-call | tf_op jit(solution)/shard_map/mlp/pallas_call | solution.py:770
  136.8 80.0 %back.1 = (bf16[2048,1536]{1,0:T(8,128)(2,1)}, f32[1024,512]{1,0:T(8,128)}, f32[16,1408]{1,0:T(8,128)}, f32[16,2,1408]{2,1,0:T(2,128)}) custom-call(f32[4,4,4,16,1408]{4,3,2,1,0:T(8,128)} %get-tuple-element.32.gd_hbm, bf16[2048,1024]{1,0:T(8,128)(2,1)} %get-tuple-element.33.n2_ref, bf16[2048,4224]{1,0:T(8,128)(2,1)} %get-tuple-element.34.act_ref, ...), custom_call_target="tpu_custom_call" | custom-call | tf_op jit(solution)/shard_map/back/pallas_call | solution.py:874
  216.7 0.0 copy-start
  216.7 1.9 copy-done
  218.6 0.0 copy-start.1
  218.6 1.6 copy-done.1
  220.2 0.0 copy-start.2
  220.2 48.8 %last.1 = (bf16[2048,1024]{1,0:T(8,128)(2,1)}, f32[8,16,64]{2,1,0:T(8,128)S(1)}, f32[16,3,8,64]{3,2,1,0:T(8,128)S(1)}) custom-call(bf16[2048,1024]{1,0:T(8,128)(2,1)} %get-tuple-element.31.n1_ref, bf16[2048,1536]{1,0:T(8,128)(2,1)} %get-tuple-element.41.g_ref.g_row, bf16[2048,1024]{1,0:T(8,128)(2,1)} %bitcast.18, ...), custom_call_target="tpu_custom_call" | custom-call | tf_op jit(solution)/shard_map/last/pallas_call | solution.py:964
  269.0 0.0 copy-done.2
  269.0 0.0 copy-start.3
  269.0 2.1 copy.19
  271.2 1.6 copy-done.3
  272.7 0.0 copy-start.4
  272.7 0.0 copy-start.5
  272.7 2.0 copy.20
  274.8 0.7 copy.21
  275.4 0.6 copy.22
  276.1 0.0 copy-done.4
  276.1 0.7 copy.23
  276.7 0.0 copy-done.5
  276.7 0.6 copy.24
Async XLA Ops:
  216.7 1.9 copy-start
  218.6 1.6 copy-start.1
  220.2 48.8 %copy-start.2 = (bf16[2048,1024]{1,0:T(8,128)(2,1)S(1)}, bf16[2048,1024]{1,0:T(8,128)(2,1)}, u32[]{:S(2)}) copy-start(bf16[2048,1024]{1,0:T(8,128)(2,1)} %get-tuple-element.30) | copy-start | bytes 12582916
  269.0 3.7 %copy-start.3 = (bf16[2048,1024]{1,0:T(8,128)(2,1)S(1)}, bf16[2048,1024]{1,0:T(8,128)(2,1)}, u32[]{:S(2)}) copy-start(bf16[2048,1024]{1,0:T(8,128)(2,1)} %get-tuple-element.45) | copy-start | bytes 12582916
  272.7 3.3 %copy-start.4 = (f32[16,2,1408]{2,1,0:T(2,128)S(1)}, f32[16,2,1408]{2,1,0:T(2,128)}, u32[]{:S(2)}) copy-start(f32[16,2,1408]{2,1,0:T(2,128)} %get-tuple-element.60) | copy-start | bytes 540676
  272.7 4.0 %copy-start.5 = (f32[16,1408]{1,0:T(8,128)S(1)}, f32[16,1408]{1,0:T(8,128)}, u32[]{:S(2)}) copy-start(f32[16,1408]{1,0:T(8,128)} %get-tuple-element.49) | copy-start | bytes 270340
where the time goes:
time: 278 us; the launch traced here: 277 us
  Pallas kernels  265 us (95%)
  local copies, waits for them, and re-layouts  11.8 us (4%)
    pallas_call x1, Pallas kernels, back(): pl.pallas_call(functools.partial(back_kernel, pairs), grid=(HEAD_STEP + b...  80 us
    pallas_call x1, Pallas kernels, front(): pl.pallas_call(front_kernel, grid=(1 + batch * pairs,), in_specs=[HBM] +...  73.8 us
    pallas_call x1, Pallas kernels, mlp(): pl.pallas_call(functools.partial(mlp_kernel, blocks), grid=(blocks + 1,),...  62.4 us
    pallas_call x1, Pallas kernels, last(): pl.pallas_call(functools.partial(last_kernel, pairs, blocks), grid=(pairs...  48.8 us
    unnamed x18, local copies, waits for them, and re-layouts  11.8 us

commit v1 on v0

--- a/solution.py
+++ b/solution.py
@@ -10,6 +10,7 @@
 
 MESH_ID = pl.DeviceIdType.MESH
 SIDE = 4
+TILE = 128
 PIECE = 16
 ORDERS = ((2, 1, 0), (1, 0, 2), (0, 2, 1))
 BOTH = ((0, 1), (1, -1))
@@ -84,7 +85,7 @@
         if half is not None and phase:
             pick[order[0]] = pl.ds(half * 2, 2)
         elif half is not None:
-            cut = width - width // 256 * 128
+            cut = width - width // (2 * TILE) * TILE
             off, width = (off + cut, width - cut) if half else (off, cut)
         return self.out.at[(*pick, slice(None), pl.ds(off, width))] if width else None
 
@@ -157,8 +158,8 @@
 class Scatter:
     SEMS = 9
 
-    def __init__(self, net, part, cols, bufs, sems, first):
-        self.net, self.part, self.cols, self.bufs, self.sems, self.first = net, part, cols, bufs, sems, first
+    def __init__(self, net, part, cols, bufs, sems, first, relays=len(PHASES)):
+        self.net, self.part, self.cols, self.bufs, self.sems, self.first, self.relays = net, part, cols, bufs, sems, first, relays
 
     @staticmethod
     def scratch(cols):
@@ -188,12 +189,14 @@
     def copy(self, phase, colour, kind, d, by):
         axis = ORDERS[colour][phase]
         buf = self.buf(colour, phase)
-        if kind == 2:
+        direct = phase >= self.relays
+        if kind == 2 and not direct:
             src = buf.at[0, d]
         elif kind:
-            src = self.block(colour, phase, self.net.shift(axis, by), 1 - d)
+            src = self.block(colour, phase, self.net.shift(axis, by), (kind + d) % 2)
         else:
             src = self.block(colour, phase, self.net.shift(axis, 2), d)
+            by = 2 if direct else by
         return pltpu.make_async_remote_copy(src, buf.at[kind, d], *self.sem(phase, kind), device_id=self.net.peer(axis, by), device_id_type=MESH_ID)
 
     def sem(self, phase, kind):
@@ -218,15 +221,17 @@
         self.start(phase, 2)
 
     def merge(self, phase):
-        for kind in (1, 2):
+        direct = phase >= self.relays
+        for kind in THREE if direct else (1, 2):
             self.wait(phase, kind, 1)
         for colour in THREE:
             buf = self.buf(colour, phase)
             for half in TWO:
                 mine = self.block(colour, phase, self.net.at[ORDERS[colour][phase]], half)
-                mine[...] = mine[...] + buf[1, 1 - half] + buf[2, half]
-        if phase + 1 < len(PHASES):
-            for kind in TWO:
+                sums = mine[...] + buf[1, 1 - half] + buf[2, half]
+                mine[...] = sums + buf[0, half] if direct else sums
+        if phase < PHASES[-1]:
+            for kind in TWO if phase + 1 < self.relays else THREE:
                 self.start(phase + 1, kind)
 
     def finish(self):
@@ -237,7 +242,7 @@
     def stages(self):
         calls = [functools.partial(self.start, 0, kind) for kind in TWO]
         for phase in PHASES:
-            calls += [functools.partial(self.relay, phase), functools.partial(self.merge, phase)]
+            calls += [functools.partial(self.relay, phase)] * (phase < self.relays) + [functools.partial(self.merge, phase)]
         return calls[:-1] + [in_order(calls[-1], self.finish)]
 
     def result(self):
@@ -245,8 +250,8 @@
 
 
 def cut_three(width, off=0, turn=0):
-    tiles = width // 128
-    sizes = [(tiles + (2 + turn - i) % 3) // 3 * 128 for i in THREE]
+    tiles, ways = width // TILE, len(THREE)
+    sizes = [(tiles + (turn - i - 1) % ways) // ways * TILE for i in THREE]
     return [(off + sum(sizes[:i]), s) for i, s in enumerate(sizes)]
 
 
@@ -266,9 +271,10 @@
 
 F32, BF16 = jnp.float32, jnp.bfloat16
 QB = 256
-LANES = 128
+LANES = TILE
 HALF = LANES // 2
 CLIP = 8.0
+BLOCK = 512
 MIB = 2**20
 
 
@@ -420,8 +426,8 @@
     return inv * (grad - mean - normed * proj)
 
 
-def params(collective_id, limit=63):
-    return pltpu.CompilerParams(collective_id=collective_id, has_side_effects=True, vmem_limit_bytes=limit * MIB)
+def params(collective_id):
+    return pltpu.CompilerParams(collective_id=collective_id, has_side_effects=True, vmem_limit_bytes=63 * MIB)
 
 
 def grid_step():
@@ -480,9 +486,9 @@
 
 CHUNK = 256
 CHUNK_STEPS = 4
-FRONT_PLAN = '014560145260124530,4,245,,13,,345,,2,,4,,3,,5,,,5'
-SCATTER_PLAN = '00,,,,,11,,,20,,,,12,,,20,1,,20,12,10,2,102,,102'
-LAST_PLAN = '00,,1,202,,31,3,,413,442,31,04,231,402,13,402,,1,403201342'
+FRONT_PLAN = '014560145260124530,,245,,134,,345,,24,,,,3,,,5,,5'
+SCATTER_PLAN = '00,,,,,1,1,,2,0,,,2,12,0,,,,12,0,1,2,012,102,102'
+LAST_PLAN = '00,,11,2,0,1,3,22,3,410,,234,4,201,3,402,1342,01,30241'
 
 
 def to_partner(net, src, dst, send, recv):
@@ -759,7 +765,7 @@
         save_grad.wait()
 
 
-def mlp(h, gy, weights, collective_id, block=512):
+def mlp(h, gy, weights, collective_id, block=BLOCK):
     rows, d = h.shape
     ff = weights.shape[1] // 3
     half = block // 2
@@ -893,7 +899,7 @@
     net = Torus()
     per = len(bufs) // (pairs + 1)
     parts = [part_out] + [part_qkv.at[j] for j in range(pairs)]
-    scatters = [Scatter(net, s, cut_three(s.shape[-1], turn=i), bufs[per * i:per * i + per], scatter_sems, i * Scatter.SEMS) for i, s in enumerate(parts)]
+    scatters = [Scatter(net, s, cut_three(s.shape[-1], turn=i), bufs[per * i:per * i + per], scatter_sems, i * Scatter.SEMS, 1 if i > pairs // 2 else len(PHASES)) for i, s in enumerate(parts)]
     calls = plan(LAST_PLAN, *(s.stages() for s in scatters))
     swap = Exchange(net, rows, ((part, got),), ((buf, gx_hbm),), sems, local_sem)
 
@@ -901,7 +907,7 @@
     def _():
         load = pltpu.make_async_copy(gout_hbm, part_out, local_sem.at[1, 0])
         load.start()
-        net.barrier(net.neighbours() + [net.partner])
+        net.barrier(net.neighbours(2) + [net.partner])
         load.wait()
 
     begin, end = halves_of(calls)
@@ -952,7 +958,7 @@
             gw_ref[:, i] = jnp.stack([t[:, cols] for t in tiles for cols in halves]).swapaxes(0, 1)
 
 
-def last(x, n1, g, gh32, w, gout, pairs, collective_id, block=512):
+def last(x, n1, g, gh32, w, gout, pairs, collective_id, block=BLOCK):
     rows, d = x.shape
     blocks = rows // block
     late = lambda n, width, by: rows_of(n, width, lambda s: jnp.clip(s - pairs - by, 0, blocks - 1))
@@ -969,9 +975,28 @@
         out_shape=[shape(BF16, rows, d), shape(F32, 2 * pairs, PIECE, HALF), shape(F32, PIECE, 3, 2 * pairs, HALF)],
         scratch_shapes=[vm(gout.shape, F32), vm((pairs,) + torus + (3 * LANES,), F32), vm((2, block, d), F32), vm((blocks, half, d), F32), vm((2, half, d), BF16),
                         dma(2, 2, blocks), dma(2, (pairs + 1) * Scatter.SEMS), dma(2, 2)] + Scatter.scratch(cut_three(gout.shape[-1])) + Scatter.scratch(cut_three(3 * LANES)) * pairs,
-        compiler_params=params(collective_id, 46),
+        compiler_params=params(collective_id),
         name='last',
     )(n1, g, x, g, gh32, w, gout)
+
+
+def hand_over_kernel(*refs):
+    count = len(refs) // 2
+    for src, dst in zip(refs[:count], refs[count:]):
+        dst[...] = src[...]
+
+
+def hand_over(wide, small, block=BLOCK):
+    rows, width = wide[0].shape
+    specs = [rows_of(block, width, lambda i: i) for v in wide] + [WHOLE for v in small]
+    return pl.pallas_call(
+        hand_over_kernel,
+        grid=(rows // block,),
+        in_specs=specs,
+        out_specs=specs,
+        out_shape=[shape(v.dtype, *v.shape) for v in wide + small],
+        name='hand_over',
+    )(*wide, *small)
 
 
 def device_step(x, grad_y, w_qkv, w_out, w_ff, w_down):
@@ -986,6 +1011,7 @@
     y, gh, gh32, acts, n2, gd = mlp(h, gy, wf, next(ids))
     g, gout, gd, gff = back(gd, n2, acts, qkv, lse, gh, wo_t, o, keep, table, batch, seq, pairs, next(ids))
     gx, gout, gqkv = last(x2, n1, g, gh32, wq, gout, pairs, next(ids))
+    y, gx, gqkv, gout, gff, gd = hand_over([y, gx], [gqkv, gout, gff, gd])
     return y.reshape(x.shape), gx.reshape(x.shape), gqkv, gout.swapaxes(1, 2), gff, gd.T
 
 

time: 278 us -> 272 us (0.978)
  local copies, waits for them, and re-layouts: 11.8 us -> 0 us
  Pallas kernels: 265 us -> 271 us
    unnamed x18 -> x0, local copies, waits for them, and re-layouts: 11.8 us -> none
    pallas_call x0 -> x1, Pallas kernels: none -> 7.31 us  [hand_over(): pl.pallas_call(hand_over_kernel, grid=(rows // block,), in_specs=specs, o...]
where the time goes in v1:
time: 272 us
  Pallas kernels  271 us (100%)
    pallas_call x1, Pallas kernels, back(): pl.pallas_call(functools.partial(back_kernel, pairs), grid=(HEAD_STEP + b...  77.8 us
    pallas_call x1, Pallas kernels, front(): pl.pallas_call(front_kernel, grid=(1 + batch * pairs,), in_specs=[HBM] +...  75 us
    pallas_call x1, Pallas kernels, mlp(): pl.pallas_call(functools.partial(mlp_kernel, blocks), grid=(blocks + 1,),...  62.4 us
    pallas_call x1, Pallas kernels, last(): pl.pallas_call(functools.partial(last_kernel, pairs, blocks), grid=(pairs...  48.9 us
    pallas_call x1, Pallas kernels, hand_over(): pl.pallas_call(hand_over_kernel, grid=(rows // block,), in_specs=specs, o...  7.31 us

profile of v1, /device:TPU:1, one launch (start us, length us, event | category | flops | bytes accessed | tf_op | source)
XLA Modules:
  0.0 272.2 jit_solution(601864983944883182)
XLA Ops:
  0.6 75.0 %front.1 = (bf16[2048,1536]{1,0:T(8,128)(2,1)}, bf16[2048,1536]{1,0:T(8,128)(2,1)}, bf16[2048,512]{1,0:T(8,128)(2,1)}, f32[2,4,2,1024]{3,2,1,0:T(2,128)}, bf16[2...) custom-call(bf16[2048,1024]{1,0:T(8,128)(2,1)} %bitcast.14, ...), custom_call_target="tpu_custom_call" | custom-call | tf_op jit(solution)/shard_map/front/pallas_call | solution.py:638
  75.6 62.4 %mlp.1 = (bf16[2048,1024]{1,0:T(8,128)(2,1)}, bf16[2048,1024]{1,0:T(8,128)(2,1)}, f32[1024,1024]{1,0:T(8,128)}, bf16[2048,4224]{1,0:T(8,128)(2,1)}, bf16[2048,10...) custom-call(bf16[2048,1024]{1,0:T(8,128)(2,1)} %get-tuple-element.34.h_ref, bf16[2048,1024]{1,0:T(8,128)(2,1)} %bitcast.16, ...), custom_call_target="tpu_custom_call" | custom-call | tf_op jit(solution)/shard_map/mlp/pallas_call | solution.py:776
  138.0 77.8 %back.1 = (bf16[2048,1536]{1,0:T(8,128)(2,1)}, f32[1024,512]{1,0:T(8,128)}, f32[16,1408]{1,0:T(8,128)}, f32[16,2,1408]{2,1,0:T(2,128)}) custom-call(f32[4,4,4,16,1408]{4,3,2,1,0:T(8,128)} %get-tuple-element.38.gd_hbm, bf16[2048,1024]{1,0:T(8,128)(2,1)} %get-tuple-element.39.n2_ref, bf16[2048,4224]{1,0:T(8,128)(2,1)} %get-tuple-element.40.act_ref, ...), custom_call_target="tpu_custom_call" | custom-call | tf_op jit(solution)/shard_map/back/pallas_call | solution.py:880
  215.8 48.9 %last.1 = (bf16[2048,1024]{1,0:T(8,128)(2,1)}, f32[8,16,64]{2,1,0:T(8,128)}, f32[16,3,8,64]{3,2,1,0:T(8,128)}) custom-call(bf16[2048,1024]{1,0:T(8,128)(2,1)} %get-tuple-element.37.n1_ref, bf16[2048,1536]{1,0:T(8,128)(2,1)} %get-tuple-element.47.g_ref.g_row, bf16[2048,1024]{1,0:T(8,128)(2,1)} %bitcast.15, bf16[2048,1536]{1,0:T(8,128)(2,1)} %get-tuple-element.47.g_ref.g_row, ...), custom_call_target="tpu_custom_call" | custom-call | tf_op jit(solution)/shard_map/last/pallas_call | solution.py:970
  264.6 7.3 %hand_over.1 = (bf16[2048,1024]{1,0:T(8,128)(2,1)}, bf16[2048,1024]{1,0:T(8,128)(2,1)}, f32[16,3,8,64]{3,2,1,0:T(8,128)}, f32[8,16,64]{2,1,0:T(8,128)}, f32[16,2,1408]{2,1,0:T(2,128)}, /*index=5*/f32[16,1408]{1,0:T(8,128)}) custom-call(bf16[2048,1024]{1,0:T(8,128)(2,1)} %get-tuple-element.36.refs_0_, bf16[2048,1024]{1,0:T(8,128)(2,1)} %get-tuple-element.51.refs_1_, ...), custom_call_target="tpu_custom_call" | custom-call | tf_op jit(solution)/shard_map/hand_over/pallas_call | solution.py:992

commit v2 on v1

--- a/solution.py
+++ b/solution.py
@@ -313,7 +313,7 @@
     masks = head_masks(True)
     key, val = k_ref[...], v_ref[...]
     causal = causal_tile(1)
-    first = head_masks(False)[0]
+    first, _ = head_masks(False)
     for lo in reversed(strips(q_ref.shape[0], QB)):
         hi = lo + QB
         query = by_head(q_ref[lo:hi, :], masks)
@@ -458,8 +458,8 @@
     return pl.BlockSpec((size, width), lambda step: (index(step), 0))
 
 
-def fixed(block, index=(0, 0)):
-    return pl.BlockSpec(block, lambda *grid: index, pipeline_mode=pl.Buffered(buffer_count=1))
+def stats_rows(seq, index):
+    return pl.BlockSpec((1, 1, 2, seq), lambda step: (*index(step), 0, 0))
 
 
 def project_pair(n1_ref, weight, cos_ref, sin_ref, qkv_ref, keep_ref):
@@ -486,7 +486,7 @@
 
 CHUNK = 256
 CHUNK_STEPS = 4
-FRONT_PLAN = '014560145260124530,,245,,134,,345,,24,,,,3,,,5,,5'
+FRONT_PLAN = '014560145260512430,,24,45,13,,345,,24,,,,3,,,5,,5'
 SCATTER_PLAN = '00,,,,,1,1,,2,0,,,2,12,0,,,,12,0,1,2,012,102,102'
 LAST_PLAN = '00,,11,2,0,1,3,22,3,410,,234,4,201,3,402,1342,01,30241'
 
@@ -639,7 +639,7 @@
         front_kernel,
         grid=(1 + batch * pairs,),
         in_specs=[HBM] + [WHOLE] * 5,
-        out_specs=[head(width), head(width), head(LANES), pl.BlockSpec((1, 1, 2, seq), lambda s: (turn(s) % batch, turn(s) // batch, 0, 0))] + [HBM] * 5,
+        out_specs=[head(width), head(width), head(LANES), stats_rows(seq, lambda s: (turn(s) % batch, turn(s) // batch))] + [HBM] * 5,
         out_shape=[shape(BF16, rows, width * pairs)] * 2 + [shape(BF16, rows, LANES * pairs), shape(F32, batch, pairs, 2, seq), shape(BF16, rows, d), shape(BF16, rows, d),
                    shape(BF16, *torus, shards[0]), shape(BF16, *torus, shards[1]), shape(BF16, *torus, shards[2] + shards[3])],
         scratch_shapes=[vm((rows, d), BF16), vm((rows, d), BF16), vm(torus + (width * pairs,), BF16), vm((PIECE, sum(shards)), BF16),
@@ -683,9 +683,13 @@
         self.results_of(at, self.net.core, act)
         self.results_of(at, 1 - self.net.core, lambda buf, rows, sem, local_sem: to_partner(self.net, buf, rows, *sem).wait_recv())
 
-
-def mlp_kernel(blocks, h_ref, gy_ref, wff_ref, wd_ref, y_hbm, gh_hbm, gh32_ref, acts_hbm, n2_ref, gd_hbm,
-               saved, grad_down, part_y, part_g, got_y, got_g, y_buf, gh_buf, h_own, gy_own, sems, local_sem, save_sem):
+    def settle_tail(self, blocks):
+        for at in TWO:
+            self.settle(blocks - len(TWO) + at)
+
+
+def mlp_kernel(blocks, h_ref, gy_ref, weights, y_hbm, gh_hbm, gh32_ref, acts_hbm, n2_ref, gd_hbm,
+               wff_ref, wd_ref, saved, grad_down, part_y, part_g, got_y, got_g, y_buf, gh_buf, h_own, gy_own, sems, local_sem, save_sem, load_sem):
     step, final = grid_step()
     rows, d = h_ref.shape
     ff = wd_ref.shape[1]
@@ -699,8 +703,19 @@
     net = Torus()
     swap = Exchange(net, rows, ((part_y, got_y), (part_g, got_g)), ((y_buf, y_hbm), (gh_buf, gh_hbm)), sems, local_sem)
 
+    def loads(i):
+        out = []
+        first, size = cut_three(ff)[i]
+        for which, (dst, at) in enumerate(((wd_ref, 2 * ff), (wff_ref, 0))):
+            cols = pl.ds((1 + which) * first, (1 + which) * size)
+            out.append(pltpu.make_async_copy(weights.at[:, pl.ds(at + cols.start, cols.size)], dst.at[:, cols], load_sem.at[which, i]))
+        return out
+
     @pl.when(step == 0)
     def _():
+        for i in THREE:
+            for copy in loads(i):
+                copy.start()
         net.barrier([net.partner])
 
     @pl.when((step > 1) & (step < blocks))
@@ -715,6 +730,11 @@
         gy = gy_ref[...]
         for j in strips(ff, QB):
             w = min(QB, ff - j)
+            if j % BLOCK == 0:
+                @pl.when(step == 0)
+                def _():
+                    for copy in loads(j // BLOCK):
+                        copy.wait()
             gact = nn(gy, wd_ref[:, j:j + w])
             for i in range(j, j + w, LANES):
                 at, mid, end = 2 * i, 2 * i + LANES, 2 * i + QB
@@ -759,9 +779,9 @@
 
     @pl.when(step == blocks)
     def _():
-        for at in (blocks - 2, blocks - 1):
-            swap.settle(at)
-            save(at).wait()
+        swap.settle_tail(blocks)
+        for at in TWO:
+            save(blocks - len(TWO) + at).wait()
         save_grad.wait()
 
 
@@ -776,13 +796,13 @@
     return pl.pallas_call(
         functools.partial(mlp_kernel, blocks),
         grid=(blocks + 1,),
-        in_specs=[row(d), row(d), fixed((d, 2 * ff)), fixed((d, ff), (0, 2))],
+        in_specs=[row(d), row(d), HBM],
         out_specs=[HBM, HBM, rows_of(half, d, lambda i: jnp.maximum(i - 1, 0)), HBM, row(d), HBM],
         out_shape=[shape(BF16, rows, d), shape(BF16, rows, d), shape(F32, rows // 2, d), shape(BF16, rows, 3 * ff), shape(BF16, rows, d), shape(F32, *torus, ff)],
-        scratch_shapes=[vm((2, block, 3 * ff), BF16), vm(torus + (ff,), F32)] + [vm((2, block, d), F32)] * 2 + [vm((blocks, half, d), F32)] * 2 + [vm((2, half, d), BF16)] * 2 + [vm((half, d), BF16)] * 2 + [dma(2, 4, blocks), dma(2, 2), dma(3)],
+        scratch_shapes=[vm((d, 2 * ff), BF16), vm((d, ff), BF16), vm((2, block, 3 * ff), BF16), vm(torus + (ff,), F32)] + [vm((2, block, d), F32)] * 2 + [vm((blocks, half, d), F32)] * 2 + [vm((2, half, d), BF16)] * 2 + [vm((half, d), BF16)] * 2 + [dma(2, 4, blocks), dma(2, 2), dma(3), dma(2, 3)],
         compiler_params=params(collective_id),
         name='mlp',
-    )(h, gy, weights, weights)
+    )(h, gy, weights)
 
 
 def accumulate(part, first, left, right):
@@ -797,8 +817,8 @@
 HEAD_STEP = (SETS - 1) * CHUNK_STEPS
 
 
-def back_kernel(pairs, gd_hbm, n2_ref, act_ref, qkv_ref, lse_ref, gh_ref, wo_ref, o_ref, keep_ref, table_ref,
-                g_ref, gw_ref, gd_ref, gff_ref, cos_ref, sin_ref, do_ref, dk_ref, dv_ref, parts, sems, load_sem, *bufs):
+def back_kernel(pairs, gd_hbm, n2_ref, act_ref, qkv_ref, lse_ref, gh_hbm, wo_hbm, o_hbm, keep_ref, table_ref,
+                g_ref, gw_ref, gd_ref, gff_ref, cos_ref, sin_ref, do_ref, dk_ref, dv_ref, gh_ref, wo_ref, o_ref, parts, sems, load_sem, *bufs):
     step, final = grid_step()
     turn = step - HEAD_STEP
     p = turn % pairs
@@ -809,10 +829,17 @@
     calls = plan(SCATTER_PLAN, *(s.stages() for s in scatters))
     begin, end = halves_of(calls, HEAD_STEP + 1)
 
+    def fetch(b):
+        rows = aligned(b * 2 * half, 2 * half)
+        return [pltpu.make_async_copy(src.at[rows], dst, load_sem.at[i]) for i, (src, dst) in enumerate(((gh_hbm, gh_ref), (o_hbm, o_ref)))]
+
+    load = pltpu.make_async_copy(gd_hbm, parts.at[0], load_sem.at[2])
+    fetch_weight = pltpu.make_async_copy(wo_hbm, wo_ref, load_sem.at[3])
+
     @pl.when(step == 0)
     def _():
-        load = pltpu.make_async_copy(gd_hbm, parts.at[0], load_sem.at[0])
-        load.start()
+        for copy in [load] + fetch(0) + [fetch_weight]:
+            copy.start()
         spread_tables(table_ref, cos_ref, sin_ref)
         net.barrier(net.neighbours())
         load.wait()
@@ -832,13 +859,15 @@
             values = values * cos_ref[lo:hi, :] - swap_halves(values) * sin_ref[lo:hi, :]
         g_ref[lo:hi, cols] = (values * keep_ref[lo:hi, cols].astype(F32)).astype(BF16)
 
-    def put_dq(lo, hi, dq):
-        put(0, lo, hi, dq * 0.125)
+    put_dq = lambda lo, hi, dq: put(0, lo, hi, dq * 0.125)
 
     @pl.when(turn >= 0)
     def _():
         @pl.when(p == 0)
         def _():
+            pl.when(turn == 0)(fetch_weight.wait)
+            for copy in fetch(turn // pairs):
+                copy.wait()
             gw_ref[...] = jnp.where(turn == 0, 0.0, gw_ref[...])
 
             def body(i):
@@ -851,21 +880,24 @@
 
             repeat(len(TWO), body)
 
+            @pl.when(turn == 0)
+            def _():
+                for copy in fetch(turn + 1):
+                    copy.start()
+
         run_at(turn, begin)
         q_ref, k_ref, v_ref = (qkv_ref.at[:, pl.ds(LANES * i, LANES)] for i in THREE)
         attend_pair_back(q_ref, k_ref, v_ref, do_ref.at[p], lse_ref.at[0, 0], dk_ref, dv_ref, put_dq)
-        seq = q_ref.shape[0]
-        put(1, 0, seq, dk_ref[...])
-        put(2, 0, seq, dv_ref[...])
+        for part, grad in ((1, dk_ref), (2, dv_ref)):
+            put(part, 0, 2 * half, grad[...])
         run_at(turn, end)
 
     @pl.when(step == final)
     def _():
         gd_ref[...], *halves = [s.result() for s in scatters]
         tiles = jnp.concatenate(halves, axis=1)
-        for i in strips(tiles.shape[1], LANES):
-            at = i // QB * LANES
-            gff_ref[:, i // LANES % 2, at:at + LANES] = tiles[:, i:i + LANES]
+        for i in range(tiles.shape[1] // LANES):
+            gff_ref[:, i % 2, lanes(i // 2)] = tiles[:, lanes(i)]
 
 
 def back(gd, n2, acts, qkv, lse, gh, wo_t, o, keep, table, batch, seq, pairs, collective_id):
@@ -876,23 +908,22 @@
     head = pl.BlockSpec((seq, 3 * LANES), lambda s: (turn(s) // pairs, turn(s) % pairs))
     late = lambda s: jnp.where(s < HEAD_STEP, s % CHUNK_STEPS, CHUNK_STEPS - 1)
     vm = pltpu.VMEM
-    per_seq = lambda width: rows_of(seq, width, lambda s: turn(s) // pairs)
     return pl.pallas_call(
         functools.partial(back_kernel, pairs),
         grid=(HEAD_STEP + batch * pairs,),
-        in_specs=[HBM, rows_of(block, d, late), pl.BlockSpec((block, ff), lambda s: (late(s), jnp.minimum(s // CHUNK_STEPS, 1))), head, pl.BlockSpec((1, 1, 2, seq), lambda s: (turn(s) // pairs, turn(s) % pairs, 0, 0)),
-                  per_seq(d), fixed(wo_t.shape), per_seq(LANES * pairs), head, WHOLE],
-        out_specs=[head, fixed(wo_t.shape), WHOLE, WHOLE],
+        in_specs=[HBM, rows_of(block, d, late), pl.BlockSpec((block, ff), lambda s: (late(s), jnp.minimum(s // CHUNK_STEPS, 1))), head, stats_rows(seq, lambda s: (turn(s) // pairs, turn(s) % pairs)),
+                  HBM, HBM, HBM, head, WHOLE],
+        out_specs=[head, WHOLE, WHOLE, WHOLE],
         out_shape=[shape(BF16, *qkv.shape), shape(F32, *wo_t.shape), shape(F32, PIECE, ff), shape(F32, PIECE, 2, ff)],
-        scratch_shapes=[vm((seq, LANES), F32)] * 2 + [vm((pairs, seq, LANES), BF16)] + [vm((seq, LANES), F32)] * 2 + [vm((SETS, SIDE, SIDE, SIDE, PIECE, ff), F32),
-                        dma(2, SETS * Scatter.SEMS), dma(1)] + [s for i in range(SETS) for s in Scatter.scratch(cut_three(ff, turn=i))],
+        scratch_shapes=[vm((seq, LANES), F32)] * 2 + [vm((pairs, seq, LANES), BF16)] + [vm((seq, LANES), F32)] * 2 + [vm((seq, d), BF16), vm(wo_t.shape, BF16), vm((seq, LANES * pairs), BF16), vm((SETS, SIDE, SIDE, SIDE, PIECE, ff), F32),
+                        dma(2, SETS * Scatter.SEMS), dma(4)] + [s for i in range(SETS) for s in Scatter.scratch(cut_three(ff, turn=i))],
         compiler_params=params(collective_id),
         name='back',
     )(gd, n2, acts, qkv, lse, gh, wo_t, o, keep, table)
 
 
-def last_kernel(pairs, blocks, n1_ref, g_ref, x_ref, g_row, gh_ref, w_ref, gout_hbm, gx_hbm, gout_ref, gw_ref,
-                part_out, part_qkv, part, got, buf, sems, scatter_sems, local_sem, *bufs):
+def last_kernel(pairs, blocks, n1_hbm, g_ref, x_ref, g_row, gh_ref, w_hbm, gout_hbm, gx_hbm, gout_ref, gw_ref,
+                n1_ref, w_ref, part_out, part_qkv, part, got, buf, sems, scatter_sems, local_sem, load_sem, *bufs):
     step, final = grid_step()
     turn = step - pairs
     rows, d = x_ref.shape
@@ -903,12 +934,16 @@
     calls = plan(LAST_PLAN, *(s.stages() for s in scatters))
     swap = Exchange(net, rows, ((part, got),), ((buf, gx_hbm),), sems, local_sem)
 
+    loads = [pltpu.make_async_copy(src, dst, load_sem.at[i]) for i, (src, dst) in enumerate(((gout_hbm, part_out), (n1_hbm, n1_ref), (w_hbm, w_ref)))]
+    pl.when(turn == 0)(loads[-1].wait)
+
     @pl.when(step == 0)
     def _():
-        load = pltpu.make_async_copy(gout_hbm, part_out, local_sem.at[1, 0])
-        load.start()
+        for copy in loads:
+            copy.start()
         net.barrier(net.neighbours(2) + [net.partner])
-        load.wait()
+        for copy in loads[:-1]:
+            copy.wait()
 
     begin, end = halves_of(calls)
     run_at(step, begin)
@@ -946,8 +981,7 @@
         for when, call in calls:
             if when > 2 * (pairs + blocks) + 1:
                 call()
-        for at in (blocks - 2, blocks - 1):
-            swap.settle(at)
+        swap.settle_tail(blocks)
         out, *sums = [s.result() for s in scatters]
         halves = slice(HALF), slice(HALF, LANES)
         for j in range(pairs):
@@ -970,11 +1004,11 @@
     return pl.pallas_call(
         functools.partial(last_kernel, pairs, blocks),
         grid=(pairs + blocks + 1,),
-        in_specs=[fixed((rows, d)), head, late(block, d, 1), late(block, g.shape[1], 0), late(half, d, 1), fixed(w.shape), HBM],
+        in_specs=[HBM, head, late(block, d, 1), late(block, g.shape[1], 0), late(half, d, 1), HBM, HBM],
         out_specs=[HBM, WHOLE, WHOLE],
         out_shape=[shape(BF16, rows, d), shape(F32, 2 * pairs, PIECE, HALF), shape(F32, PIECE, 3, 2 * pairs, HALF)],
-        scratch_shapes=[vm(gout.shape, F32), vm((pairs,) + torus + (3 * LANES,), F32), vm((2, block, d), F32), vm((blocks, half, d), F32), vm((2, half, d), BF16),
-                        dma(2, 2, blocks), dma(2, (pairs + 1) * Scatter.SEMS), dma(2, 2)] + Scatter.scratch(cut_three(gout.shape[-1])) + Scatter.scratch(cut_three(3 * LANES)) * pairs,
+        scratch_shapes=[vm((rows, d), BF16), vm(w.shape, BF16), vm(gout.shape, F32), vm((pairs,) + torus + (3 * LANES,), F32), vm((2, block, d), F32), vm((blocks, half, d), F32), vm((2, half, d), BF16),
+                        dma(2, 2, blocks), dma(2, (pairs + 1) * Scatter.SEMS), dma(1, 2), dma(3)] + Scatter.scratch(cut_three(gout.shape[-1])) + Scatter.scratch(cut_three(3 * LANES)) * pairs,
         compiler_params=params(collective_id),
         name='last',
     )(n1, g, x, g, gh32, w, gout)
@@ -986,7 +1020,7 @@
         dst[...] = src[...]
 
 
-def hand_over(wide, small, block=BLOCK):
+def hand_over(wide, small, block=QB):
     rows, width = wide[0].shape
     specs = [rows_of(block, width, lambda i: i) for v in wide] + [WHOLE for v in small]
     return pl.pallas_call(
@@ -1004,7 +1038,7 @@
     heads, head = w_qkv.shape[2:]
     pairs = heads // 2
     table = jnp.asarray(tables(seq, head))
-    ids = iter(range(4))
+    ids = iter(range(SIDE))
     x2, gy = (v.reshape(batch * seq, d) for v in (x, grad_y))
     qkv, keep, o, lse, h, n1, *weights = front(x2, w_qkv, w_out.swapaxes(1, 2), w_ff, w_down.T, table, batch, seq, next(ids))
     wq, wo_t, wf = (w.reshape(d, w.shape[-1]) for w in weights)

time: 272 us -> 279 us (1.026)
  Pallas kernels: 271 us -> 277 us
    pallas_call x1, Pallas kernels: 75 us -> 78.3 us  [front(): pl.pallas_call(front_kernel, grid=(1 + batch * pairs,), in_specs=[HBM] +...]
    pallas_call x1, Pallas kernels: 62.4 us -> 65.6 us  [mlp(): pl.pallas_call(functools.partial(mlp_kernel, blocks), grid=(blocks + 1,),...]
where the time goes in v2:
time: 279 us; the launch traced here: 278 us
  Pallas kernels  277 us (99%)
    pallas_call x1, Pallas kernels, front(): pl.pallas_call(front_kernel, grid=(1 + batch * pairs,), in_specs=[HBM] +...  78.3 us
    pallas_call x1, Pallas kernels, back(): pl.pallas_call(functools.partial(back_kernel, pairs), grid=(HEAD_STEP + b...  76.4 us
    pallas_call x1, Pallas kernels, mlp(): pl.pallas_call(functools.partial(mlp_kernel, blocks), grid=(blocks + 1,),...  65.6 us
    pallas_call x1, Pallas kernels, last(): pl.pallas_call(functools.partial(last_kernel, pairs, blocks), grid=(pairs...  47.7 us
    pallas_call x1, Pallas kernels, hand_over(): pl.pallas_call(hand_over_kernel, grid=(rows // block,), in_specs=specs, o...  9.19 us

profile of v2, /device:TPU:1, one launch (start us, length us, event | category | flops | bytes accessed | tf_op | source)
XLA Modules:
  0.0 278.1 jit_solution(8503428781079040535)
XLA Ops:
  0.6 78.3 %front.1 = (bf16[2048,1536]{1,0:T(8,128)(2,1)}, bf16[2048,1536]{1,0:T(8,128)(2,1)}, bf16[2048,512]{1,0:T(8,128)(2,1)}, f32[2,4,2,1024]{3,2,1,0:T(2,128)}, bf16[2...) custom-call(bf16[2048,1024]{1,0:T(8,128)(2,1)} %bitcast.12, ...), custom_call_target="tpu_custom_call" | custom-call | tf_op jit(solution)/shard_map/front/pallas_call | solution.py:638
  78.9 65.6 %mlp.1 = (bf16[2048,1024]{1,0:T(8,128)(2,1)}, bf16[2048,1024]{1,0:T(8,128)(2,1)}, f32[1024,1024]{1,0:T(8,128)}, bf16[2048,4224]{1,0:T(8,128)(2,1)}, bf16[2048,10...) custom-call(bf16[2048,1024]{1,0:T(8,128)(2,1)} %get-tuple-element.34.h_ref, bf16[2048,1024]{1,0:T(8,128)(2,1)} %bitcast.15, ...), custom_call_target="tpu_custom_call" | custom-call | tf_op jit(solution)/shard_map/mlp/pallas_call | solution.py:796
  144.5 76.4 %back.1 = (bf16[2048,1536]{1,0:T(8,128)(2,1)}, f32[1024,512]{1,0:T(8,128)}, f32[16,1408]{1,0:T(8,128)}, f32[16,2,1408]{2,1,0:T(2,128)}) custom-call(f32[4,4,4,16,1408]{4,3,2,1,0:T(8,128)} %get-tuple-element.38.gd_hbm, bf16[2048,1024]{1,0:T(8,128)(2,1)} %get-tuple-element.39.n2_ref, bf16[2048,4224]{1,0:T(8,128)(2,1)} %get-tuple-element.40.act_ref, ...), custom_call_target="tpu_custom_call" | custom-call | tf_op jit(solution)/shard_map/back/pallas_call | solution.py:911
  220.9 47.7 %last.1 = (bf16[2048,1024]{1,0:T(8,128)(2,1)}, f32[8,16,64]{2,1,0:T(8,128)}, f32[16,3,8,64]{3,2,1,0:T(8,128)}) custom-call(bf16[2048,1024]{1,0:T(8,128)(2,1)} %get-tuple-element.37.n1_hbm, bf16[2048,1536]{1,0:T(8,128)(2,1)} %get-tuple-element.47.g_ref.g_row, bf16[2048,1024]{1,0:T(8,128)(2,1)} %bitcast.13, bf16[2048,1536]{1,0:T(8,128)(2,1)} %get-tuple-element.47.g_ref.g_row, ...), custom_call_target="tpu_custom_call" | custom-call | tf_op jit(solution)/shard_map/last/pallas_call | solution.py:1004
  268.7 9.2 %hand_over.1 = (bf16[2048,1024]{1,0:T(8,128)(2,1)}, bf16[2048,1024]{1,0:T(8,128)(2,1)}, f32[16,3,8,64]{3,2,1,0:T(8,128)}, f32[8,16,64]{2,1,0:T(8,128)}, f32[16,2,1408]{2,1,0:T(2,128)}, /*index=5*/f32[16,1408]{1,0:T(8,128)}) custom-call(bf16[2048,1024]{1,0:T(8,128)(2,1)} %get-tuple-element.36.refs_0_, bf16[2048,1024]{1,0:T(8,128)(2,1)} %get-tuple-element.51.refs_1_, ...), custom_call_target="tpu_custom_call" | custom-call | tf_op jit(solution)/shard_map/hand_over/pallas_call | solution.py:1026

commit v3 on v2

--- a/solution.py
+++ b/solution.py
@@ -486,7 +486,7 @@
 
 CHUNK = 256
 CHUNK_STEPS = 4
-FRONT_PLAN = '014560145260512430,,24,45,13,,345,,24,,,,3,,,5,,5'
+FRONT_PLAN = '014560145260512430,,4,5,1234,,345,,24,,,,3,,,5,,5'
 SCATTER_PLAN = '00,,,,,1,1,,2,0,,,2,12,0,,,,12,0,1,2,012,102,102'
 LAST_PLAN = '00,,11,2,0,1,3,22,3,410,,234,4,201,3,402,1342,01,30241'
 
@@ -703,20 +703,15 @@
     net = Torus()
     swap = Exchange(net, rows, ((part_y, got_y), (part_g, got_g)), ((y_buf, y_hbm), (gh_buf, gh_hbm)), sems, local_sem)
 
-    def loads(i):
-        out = []
-        first, size = cut_three(ff)[i]
-        for which, (dst, at) in enumerate(((wd_ref, 2 * ff), (wff_ref, 0))):
-            cols = pl.ds((1 + which) * first, (1 + which) * size)
-            out.append(pltpu.make_async_copy(weights.at[:, pl.ds(at + cols.start, cols.size)], dst.at[:, cols], load_sem.at[which, i]))
-        return out
+    loads = [pltpu.make_async_copy(weights.at[:, pl.ds(at, dst.shape[1])], dst, load_sem.at[i]) for i, (dst, at) in enumerate(((wd_ref, 2 * ff), (wff_ref, 0)))]
 
     @pl.when(step == 0)
     def _():
-        for i in THREE:
-            for copy in loads(i):
-                copy.start()
+        for copy in loads:
+            copy.start()
         net.barrier([net.partner])
+        for copy in loads:
+            copy.wait()
 
     @pl.when((step > 1) & (step < blocks))
     def _():
@@ -730,11 +725,6 @@
         gy = gy_ref[...]
         for j in strips(ff, QB):
             w = min(QB, ff - j)
-            if j % BLOCK == 0:
-                @pl.when(step == 0)
-                def _():
-                    for copy in loads(j // BLOCK):
-                        copy.wait()
             gact = nn(gy, wd_ref[:, j:j + w])
             for i in range(j, j + w, LANES):
                 at, mid, end = 2 * i, 2 * i + LANES, 2 * i + QB
@@ -799,7 +789,7 @@
         in_specs=[row(d), row(d), HBM],
         out_specs=[HBM, HBM, rows_of(half, d, lambda i: jnp.maximum(i - 1, 0)), HBM, row(d), HBM],
         out_shape=[shape(BF16, rows, d), shape(BF16, rows, d), shape(F32, rows // 2, d), shape(BF16, rows, 3 * ff), shape(BF16, rows, d), shape(F32, *torus, ff)],
-        scratch_shapes=[vm((d, 2 * ff), BF16), vm((d, ff), BF16), vm((2, block, 3 * ff), BF16), vm(torus + (ff,), F32)] + [vm((2, block, d), F32)] * 2 + [vm((blocks, half, d), F32)] * 2 + [vm((2, half, d), BF16)] * 2 + [vm((half, d), BF16)] * 2 + [dma(2, 4, blocks), dma(2, 2), dma(3), dma(2, 3)],
+        scratch_shapes=[vm((d, 2 * ff), BF16), vm((d, ff), BF16), vm((2, block, 3 * ff), BF16), vm(torus + (ff,), F32)] + [vm((2, block, d), F32)] * 2 + [vm((blocks, half, d), F32)] * 2 + [vm((2, half, d), BF16)] * 2 + [vm((half, d), BF16)] * 2 + [dma(2, 4, blocks), dma(2, 2), dma(3), dma(2)],
         compiler_params=params(collective_id),
         name='mlp',
     )(h, gy, weights)
@@ -1020,7 +1010,7 @@
         dst[...] = src[...]
 
 
-def hand_over(wide, small, block=QB):
+def hand_over(wide, small, block=2 * BLOCK):
     rows, width = wide[0].shape
     specs = [rows_of(block, width, lambda i: i) for v in wide] + [WHOLE for v in small]
     return pl.pallas_call(
@@ -1029,6 +1019,7 @@
         in_specs=specs,
         out_specs=specs,
         out_shape=[shape(v.dtype, *v.shape) for v in wide + small],
+        compiler_params=pltpu.CompilerParams(vmem_limit_bytes=40 * MIB),
         name='hand_over',
     )(*wide, *small)
 

time: 279 us -> 273 us (0.978)
  Pallas kernels: 277 us -> 266 us
  local copies, waits for them, and re-layouts: 0 us -> 6.14 us
    unnamed x0 -> x12, local copies, waits for them, and re-layouts: none -> 6.14 us
    pallas_call x1, Pallas kernels: 9.19 us -> 3.73 us  [hand_over(): pl.pallas_call(hand_over_kernel, grid=(rows // block,), in_specs=specs, o...]
    pallas_call x1, Pallas kernels: 78.3 us -> 74.5 us  [front(): pl.pallas_call(front_kernel, grid=(1 + batch * pairs,), in_specs=[HBM] +...]
where the time goes in v3:
time: 273 us
  Pallas kernels  266 us (97%)
  local copies, waits for them, and re-layouts  6.14 us (2%)
    pallas_call x1, Pallas kernels, back(): pl.pallas_call(functools.partial(back_kernel, pairs), grid=(HEAD_STEP + b...  76.7 us
    pallas_call x1, Pallas kernels, front(): pl.pallas_call(front_kernel, grid=(1 + batch * pairs,), in_specs=[HBM] +...  74.5 us
    pallas_call x1, Pallas kernels, mlp(): pl.pallas_call(functools.partial(mlp_kernel, blocks), grid=(blocks + 1,),...  63.1 us
    pallas_call x1, Pallas kernels, last(): pl.pallas_call(functools.partial(last_kernel, pairs, blocks), grid=(pairs...  47.9 us
    unnamed x12, local copies, waits for them, and re-layouts  6.14 us

profile of v3, /device:TPU:1, one launch (start us, length us, event | category | flops | bytes accessed | tf_op | source)
XLA Modules:
  0.0 272.9 jit_solution(869490467159710303)
XLA Ops:
  0.6 74.5 %front.1 = (bf16[2048,1536]{1,0:T(8,128)(2,1)}, bf16[2048,1536]{1,0:T(8,128)(2,1)}, bf16[2048,512]{1,0:T(8,128)(2,1)}, f32[2,4,2,1024]{3,2,1,0:T(2,128)}, bf16[2...) custom-call(bf16[2048,1024]{1,0:T(8,128)(2,1)} %bitcast.12, ...), custom_call_target="tpu_custom_call" | custom-call | tf_op jit(solution)/shard_map/front/pallas_call | solution.py:638
  75.1 63.1 %mlp.1 = (bf16[2048,1024]{1,0:T(8,128)(2,1)}, bf16[2048,1024]{1,0:T(8,128)(2,1)}, f32[1024,1024]{1,0:T(8,128)}, bf16[2048,4224]{1,0:T(8,128)(2,1)}, bf16[2048,10...) custom-call(bf16[2048,1024]{1,0:T(8,128)(2,1)} %get-tuple-element.34.h_ref, bf16[2048,1024]{1,0:T(8,128)(2,1)} %bitcast.15, ...), custom_call_target="tpu_custom_call" | custom-call | tf_op jit(solution)/shard_map/mlp/pallas_call | solution.py:786
  138.3 76.7 %back.1 = (bf16[2048,1536]{1,0:T(8,128)(2,1)}, f32[1024,512]{1,0:T(8,128)}, f32[16,1408]{1,0:T(8,128)}, f32[16,2,1408]{2,1,0:T(2,128)}) custom-call(f32[4,4,4,16,1408]{4,3,2,1,0:T(8,128)} %get-tuple-element.38.gd_hbm, bf16[2048,1024]{1,0:T(8,128)(2,1)} %get-tuple-element.39.n2_ref, bf16[2048,4224]{1,0:T(8,128)(2,1)} %get-tuple-element.40.act_ref, ...), custom_call_target="tpu_custom_call" | custom-call | tf_op jit(solution)/shard_map/back/pallas_call | solution.py:901
  214.9 0.0 copy-start.3
  214.9 0.0 copy-start.4
  214.9 47.9 %last.1 = (bf16[2048,1024]{1,0:T(8,128)(2,1)}, f32[8,16,64]{2,1,0:T(8,128)}, f32[16,3,8,64]{3,2,1,0:T(8,128)}) custom-call(bf16[2048,1024]{1,0:T(8,128)(2,1)} %get-tuple-element.37.n1_hbm, bf16[2048,1536]{1,0:T(8,128)(2,1)} %get-tuple-element.47.g_ref.g_row, bf16[2048,1024]{1,0:T(8,128)(2,1)} %bitcast.13, bf16[2048,1536]{1,0:T(8,128)(2,1)} %get-tuple-element.47.g_ref.g_row, ...), custom_call_target="tpu_custom_call" | custom-call | tf_op jit(solution)/shard_map/last/pallas_call | solution.py:994
  262.8 0.0 copy-done.3
  262.9 0.0 copy-done.4
  262.9 0.0 copy-start
  262.9 2.2 copy-done
  265.1 0.0 copy-start.1
  265.1 2.2 copy-done.1
  267.2 0.0 copy-start.2
  267.2 0.9 copy-done.2
  268.2 0.0 copy-start.5
  268.2 0.8 copy-done.5
  269.0 3.7 %hand_over.1 = (bf16[2048,1024]{1,0:T(8,128)(2,1)}, bf16[2048,1024]{1,0:T(8,128)(2,1)}, f32[16,3,8,64]{3,2,1,0:T(8,128)}, f32[8,16,64]{2,1,0:T(8,128)}, f32[16,2,1408]{2,1,0:T(2,128)}, /*index=5*/f32[16,1408]{1,0:T(8,128)}) custom-call(bf16[2048,1024]{1,0:T(8,128)(2,1)S(1)} %copy-done, bf16[2048,1024]{1,0:T(8,128)(2,1)S(1)} %copy-done.1, ...), custom_call_target="tpu_custom_call" | custom-call | tf_op jit(solution)/shard_map/hand_over/pallas_call | solution.py:1016
Async XLA Ops:
  214.9 47.9 %copy-start.3 = (f32[16,2,1408]{2,1,0:T(2,128)S(1)}, f32[16,2,1408]{2,1,0:T(2,128)}, u32[]{:S(2)}) copy-start(f32[16,2,1408]{2,1,0:T(2,128)} %get-tuple-element.54.refs_4_) | copy-start | bytes 540676
  214.9 47.9 %copy-start.4 = (f32[16,1408]{1,0:T(8,128)S(1)}, f32[16,1408]{1,0:T(8,128)}, u32[]{:S(2)}) copy-start(f32[16,1408]{1,0:T(8,128)} %get-tuple-element.55.refs_5_) | copy-start | bytes 270340
  262.9 2.2 copy-start
  265.1 2.2 copy-start.1
  267.2 0.9 copy-start.2
  268.2 0.8 copy-start.5

commit v4 on v3

--- a/solution.py
+++ b/solution.py
@@ -661,9 +661,12 @@
         part, got = self.partials[which]
         return to_partner(self.net, part.at[at % 2, self.half(1 - self.net.core)], got.at[at], *pair_of(self.sems, which, at))
 
+    def arrive(self, at):
+        for which in range(len(self.partials)):
+            self.part(which, at).wait()
+
     def total(self, which, at):
         part, got = self.partials[which]
-        self.part(which, at).wait()
         return part[at % 2, self.half(self.net.core), :] + got[at]
 
     def results_of(self, at, core, act):
@@ -742,11 +745,8 @@
                 part[step % 2, :, j:j + QB] = nt(left[...], right[j:j + QB, :])
             swap.part(which, step).start()
         save(step).start()
-        accumulate(grad_down, step == 0, gy, act)
-
-    @pl.when(step == blocks - 1)
-    def _():
-        save_grad.start()
+
+    done = (step + blocks) % (blocks + 1)
 
     @pl.when(step > 2)
     def _():
@@ -754,13 +754,29 @@
 
     @pl.when(step > 0)
     def _():
-        done = step - 1
+        swap.arrive(done)
+
+    def combine():
         hidden = h_own[...].astype(F32)
         normed, inv = norm_rows(hidden)
         y_buf[done % 2] = (hidden + swap.total(0, done)).astype(BF16)
         gh = gy_own[...].astype(F32) + norm_grad(swap.total(1, done), normed, inv)
         gh32_ref[...] = gh
         gh_buf[done % 2] = gh.astype(BF16)
+
+    @pl.when(step < blocks)
+    def _():
+        accumulate(grad_down, step == 0, gy_ref[...], act)
+        combine()
+
+    @pl.when(step == blocks - 1)
+    def _():
+        save_grad.start()
+
+    pl.when(step == blocks)(combine)
+
+    @pl.when(step > 0)
+    def _():
         swap.publish(done)
 
     own = swap.half(net.core)
@@ -789,7 +805,7 @@
         in_specs=[row(d), row(d), HBM],
         out_specs=[HBM, HBM, rows_of(half, d, lambda i: jnp.maximum(i - 1, 0)), HBM, row(d), HBM],
         out_shape=[shape(BF16, rows, d), shape(BF16, rows, d), shape(F32, rows // 2, d), shape(BF16, rows, 3 * ff), shape(BF16, rows, d), shape(F32, *torus, ff)],
-        scratch_shapes=[vm((d, 2 * ff), BF16), vm((d, ff), BF16), vm((2, block, 3 * ff), BF16), vm(torus + (ff,), F32)] + [vm((2, block, d), F32)] * 2 + [vm((blocks, half, d), F32)] * 2 + [vm((2, half, d), BF16)] * 2 + [vm((half, d), BF16)] * 2 + [dma(2, 4, blocks), dma(2, 2), dma(3), dma(2)],
+        scratch_shapes=[vm((d, 2 * ff), BF16), vm((d, ff), BF16), vm((2, block, 3 * ff), BF16), vm(torus + (ff,), F32)] + [vm((2, block, d), F32)] * 2 + [vm((blocks + 1, half, d), F32)] * 2 + [vm((2, half, d), BF16)] * 2 + [vm((half, d), BF16)] * 2 + [dma(2, 4, blocks), dma(2, 2), dma(3), dma(2)],
         compiler_params=params(collective_id),
         name='mlp',
     )(h, gy, weights)
@@ -949,8 +965,11 @@
 
     @pl.when((turn >= 0) & (turn < blocks))
     def _():
-        for j in strips(d, QB):
-            part[turn % 2, :, j:j + QB] = nt(g_row[...], w_ref[j:j + QB, :])
+        def body(i):
+            cols = aligned(i * QB, QB)
+            part[turn % 2, :, cols] = nt(g_row[...], w_ref[cols, :])
+
+        repeat(d // QB, body)
         swap.part(0, turn).start()
 
     run_at(step, end)
@@ -962,6 +981,7 @@
     @pl.when(turn > 0)
     def _():
         done = turn - 1
+        swap.arrive(done)
         normed, inv = norm_rows(x_ref[swap.half(net.core), :].astype(F32))
         buf[done % 2] = (gh_ref[...] + norm_grad(swap.total(0, done), normed, inv)).astype(BF16)
         swap.publish(done)
@@ -1019,7 +1039,7 @@
         in_specs=specs,
         out_specs=specs,
         out_shape=[shape(v.dtype, *v.shape) for v in wide + small],
-        compiler_params=pltpu.CompilerParams(vmem_limit_bytes=40 * MIB),
+        compiler_params=pltpu.CompilerParams(vmem_limit_bytes=63 * MIB),
         name='hand_over',
     )(*wide, *small)
 

time: 273 us -> 268 us (0.982)
  local copies, waits for them, and re-layouts: 6.14 us -> 0 us
    unnamed x12 -> x0, local copies, waits for them, and re-layouts: 6.14 us -> none
where the time goes in v4:
time: 268 us
  Pallas kernels  267 us (100%)
    pallas_call x1, Pallas kernels, back(): pl.pallas_call(functools.partial(back_kernel, pairs), grid=(HEAD_STEP + b...  76.8 us
    pallas_call x1, Pallas kernels, front(): pl.pallas_call(front_kernel, grid=(1 + batch * pairs,), in_specs=[HBM] +...  74.5 us
    pallas_call x1, Pallas kernels, mlp(): pl.pallas_call(functools.partial(mlp_kernel, blocks), grid=(blocks + 1,),...  62.2 us
    pallas_call x1, Pallas kernels, last(): pl.pallas_call(functools.partial(last_kernel, pairs, blocks), grid=(pairs...  47.7 us
    pallas_call x1, Pallas kernels, hand_over(): pl.pallas_call(hand_over_kernel, grid=(rows // block,), in_specs=specs, o...  6.07 us

profile of v4, /device:TPU:1, one launch (start us, length us, event | category | flops | bytes accessed | tf_op | source)
XLA Modules:
  0.0 268.1 jit_solution(16398585909514900627)
XLA Ops:
  0.6 74.5 %front.1 = (bf16[2048,1536]{1,0:T(8,128)(2,1)}, bf16[2048,1536]{1,0:T(8,128)(2,1)}, bf16[2048,512]{1,0:T(8,128)(2,1)}, f32[2,4,2,1024]{3,2,1,0:T(2,128)}, bf16[2...) custom-call(bf16[2048,1024]{1,0:T(8,128)(2,1)} %bitcast.12, ...), custom_call_target="tpu_custom_call" | custom-call | tf_op jit(solution)/shard_map/front/pallas_call | solution.py:638
  75.1 62.2 %mlp.1 = (bf16[2048,1024]{1,0:T(8,128)(2,1)}, bf16[2048,1024]{1,0:T(8,128)(2,1)}, f32[1024,1024]{1,0:T(8,128)}, bf16[2048,4224]{1,0:T(8,128)(2,1)}, bf16[2048,10...) custom-call(bf16[2048,1024]{1,0:T(8,128)(2,1)} %get-tuple-element.34.h_ref, bf16[2048,1024]{1,0:T(8,128)(2,1)} %bitcast.15, ...), custom_call_target="tpu_custom_call" | custom-call | tf_op jit(solution)/shard_map/mlp/pallas_call | solution.py:802
  137.3 76.8 %back.1 = (bf16[2048,1536]{1,0:T(8,128)(2,1)}, f32[1024,512]{1,0:T(8,128)}, f32[16,1408]{1,0:T(8,128)}, f32[16,2,1408]{2,1,0:T(2,128)}) custom-call(f32[4,4,4,16,1408]{4,3,2,1,0:T(8,128)} %get-tuple-element.38.gd_hbm, bf16[2048,1024]{1,0:T(8,128)(2,1)} %get-tuple-element.39.n2_ref, bf16[2048,4224]{1,0:T(8,128)(2,1)} %get-tuple-element.40.act_ref, ...), custom_call_target="tpu_custom_call" | custom-call | tf_op jit(solution)/shard_map/back/pallas_call | solution.py:917
  214.2 47.7 %last.1 = (bf16[2048,1024]{1,0:T(8,128)(2,1)}, f32[8,16,64]{2,1,0:T(8,128)}, f32[16,3,8,64]{3,2,1,0:T(8,128)}) custom-call(bf16[2048,1024]{1,0:T(8,128)(2,1)} %get-tuple-element.37.n1_hbm, bf16[2048,1536]{1,0:T(8,128)(2,1)} %get-tuple-element.47.g_ref.g_row, bf16[2048,1024]{1,0:T(8,128)(2,1)} %bitcast.13, bf16[2048,1536]{1,0:T(8,128)(2,1)} %get-tuple-element.47.g_ref.g_row, ...), custom_call_target="tpu_custom_call" | custom-call | tf_op jit(solution)/shard_map/last/pallas_call | solution.py:1014
  261.8 6.1 %hand_over.1 = (bf16[2048,1024]{1,0:T(8,128)(2,1)}, bf16[2048,1024]{1,0:T(8,128)(2,1)}, f32[16,3,8,64]{3,2,1,0:T(8,128)}, f32[8,16,64]{2,1,0:T(8,128)}, f32[16,2,1408]{2,1,0:T(2,128)}, /*index=5*/f32[16,1408]{1,0:T(8,128)}) custom-call(bf16[2048,1024]{1,0:T(8,128)(2,1)} %get-tuple-element.36.refs_0_, bf16[2048,1024]{1,0:T(8,128)(2,1)} %get-tuple-element.51.refs_1_, ...), custom_call_target="tpu_custom_call" | custom-call | tf_op jit(solution)/shard_map/hand_over/pallas_call | solution.py:1036

commit v5 on v4

--- a/solution.py
+++ b/solution.py
@@ -273,6 +273,7 @@
 QB = 256
 LANES = TILE
 HALF = LANES // 2
+PAIR = 3 * LANES
 CLIP = 8.0
 BLOCK = 512
 MIB = 2**20
@@ -495,8 +496,8 @@
     return pltpu.make_async_remote_copy(src, dst, send, recv, device_id=net.partner, device_id_type=MESH_ID)
 
 
-def front_kernel(x_hbm, qkv_shard, out_shard, ff_shard, down_shard, table_ref, qkv_ref, keep_ref, o_ref, lse_ref, h_hbm, n1_hbm, wq_hbm, wo_hbm, wf_hbm,
-                 x_all, n1, w, shards, o_all, part, got, h_buf, wo, sems, gather_sems, load_sem, h_sem, cos_ref, sin_ref, o_buf):
+def front_kernel(x_hbm, qkv_shard, out_shard, ff_shard, down_shard, table_ref, qkv_hbm, keep_hbm, o_hbm, lse_ref, h_hbm, n1_hbm, wq_hbm, wo_hbm, wf_hbm,
+                 x_all, n1, w, shards, o_all, part, got, h_buf, wo, sems, gather_sems, load_sem, h_sem, cos_ref, sin_ref, o_buf, qkv_all, keep_all, store_sem):
     step, last = grid_step()
     turn = step - 1
     batch, pairs, seq = o_all.shape[:3]
@@ -505,7 +506,7 @@
     chunks = seq // CHUNK
     ff = down_shard.shape[1]
     net = Torus()
-    width = 3 * LANES
+    width = PAIR
     heads_end, out_end = width * pairs, (width + LANES) * pairs
     places = [(w, cut_three(width, width * j), 0) for j in range(pairs)] + [
               (wo_hbm, cut_three(LANES * pairs), heads_end), (wf_hbm, cut_three(3 * ff), out_end)]
@@ -558,13 +559,27 @@
     begin, end = halves_of(calls, 1)
     run_at(turn, begin)
 
+    def store(b, p):
+        out = []
+        for i, (src, dst) in enumerate(((qkv_all.at[b], qkv_hbm), (keep_all.at[b], keep_hbm), (o_all.at[b, p], o_hbm))):
+            size = src.shape[-1]
+            out.append(pltpu.make_async_copy(src, dst.at[aligned(b * seq, seq), aligned(p * size, size)], store_sem.at[i, b]))
+        return out
+
+    @pl.when(turn >= batch)
+    def _():
+        for copy in store(b, p - 1):
+            copy.wait()
+
     @pl.when(turn >= 0)
     def _():
+        qkv_ref, keep_ref = qkv_all.at[b], keep_all.at[b]
         weight = w[:, :, :, :, pl.ds(pl.multiple_of(width * p, LANES), width)].reshape(n1.shape[1], width)
         project_pair(n1.at[aligned(b * seq, seq)], weight, cos_ref, sin_ref, qkv_ref, keep_ref)
         q_ref, k_ref, v_ref = (qkv_ref.at[:, pl.ds(LANES * i, LANES)] for i in THREE)
-        attend_pair(q_ref, k_ref, v_ref, o_ref, lse_ref.at[0, 0])
-        o_all[b, p] = o_ref[...]
+        attend_pair(q_ref, k_ref, v_ref, o_all.at[b, p], lse_ref.at[0, 0])
+        for copy in store(b, p):
+            copy.start()
 
     run_at(turn, end)
 
@@ -610,6 +625,9 @@
                 h_copy(b, c, net.core).wait_send()
                 h_local(b, c).wait()
                 h_copy(b, c, 1 - net.core).wait_recv()
+        for b in range(batch):
+            for copy in store(b, pairs - 1):
+                copy.wait()
         for i in range(CHUNK_STEPS):
             save(i).wait()
         save_weight.wait()
@@ -628,23 +646,22 @@
 def front(x, qkv_shard, out_shard, ff_shard, down_shard, table, batch, seq, collective_id):
     pairs = len(out_shard) // 2
     rows, d = x.shape
-    width = 3 * LANES
+    width = PAIR
     chunks = seq // CHUNK
     vm = pltpu.VMEM
     torus = (SIDE, SIDE, SIDE, PIECE)
     shards = [s.size // PIECE for s in (qkv_shard, out_shard, ff_shard, down_shard)]
     turn = lambda s: jnp.maximum(s - 1, 0)
-    head = lambda width: pl.BlockSpec((seq, width), lambda s: (turn(s) % batch, turn(s) // batch))
     return pl.pallas_call(
         front_kernel,
         grid=(1 + batch * pairs,),
         in_specs=[HBM] + [WHOLE] * 5,
-        out_specs=[head(width), head(width), head(LANES), stats_rows(seq, lambda s: (turn(s) % batch, turn(s) // batch))] + [HBM] * 5,
+        out_specs=[HBM] * 3 + [stats_rows(seq, lambda s: (turn(s) % batch, turn(s) // batch))] + [HBM] * 5,
         out_shape=[shape(BF16, rows, width * pairs)] * 2 + [shape(BF16, rows, LANES * pairs), shape(F32, batch, pairs, 2, seq), shape(BF16, rows, d), shape(BF16, rows, d),
                    shape(BF16, *torus, shards[0]), shape(BF16, *torus, shards[1]), shape(BF16, *torus, shards[2] + shards[3])],
         scratch_shapes=[vm((rows, d), BF16), vm((rows, d), BF16), vm(torus + (width * pairs,), BF16), vm((PIECE, sum(shards)), BF16),
                         vm((batch, pairs, seq, LANES), BF16), vm((batch, seq, d), F32), vm((batch, chunks, CHUNK // 2, d), F32), vm((batch, chunks, CHUNK // 2, d), BF16),
-                        vm(torus + (shards[1],), BF16), dma(2, 2, batch, chunks), dma(2, (pairs + 2) * Gather.SEMS), dma(CHUNK_STEPS + 1), dma(batch, chunks)] + [vm((seq, LANES), F32)] * 2 + [vm((seq, LANES * pairs), BF16)],
+                        vm(torus + (shards[1],), BF16), dma(2, 2, batch, chunks), dma(2, (pairs + 2) * Gather.SEMS), dma(CHUNK_STEPS + 1), dma(batch, chunks)] + [vm((seq, LANES), F32)] * 2 + [vm((seq, LANES * pairs), BF16)] + [vm((batch, seq, width), BF16)] * 2 + [dma(3, batch)],
         compiler_params=params(collective_id),
         name='front',
     )(x, qkv_shard, out_shard, ff_shard, down_shard, table)
@@ -911,7 +928,7 @@
     ff = acts.shape[1] // SETS
     block = rows // CHUNK_STEPS
     turn = lambda s: jnp.maximum(s - HEAD_STEP, 0)
-    head = pl.BlockSpec((seq, 3 * LANES), lambda s: (turn(s) // pairs, turn(s) % pairs))
+    head = pl.BlockSpec((seq, PAIR), lambda s: (turn(s) // pairs, turn(s) % pairs))
     late = lambda s: jnp.where(s < HEAD_STEP, s % CHUNK_STEPS, CHUNK_STEPS - 1)
     vm = pltpu.VMEM
     return pl.pallas_call(
@@ -1006,7 +1023,7 @@
     rows, d = x.shape
     blocks = rows // block
     late = lambda n, width, by: rows_of(n, width, lambda s: jnp.clip(s - pairs - by, 0, blocks - 1))
-    head = pl.BlockSpec((rows, 3 * LANES), lambda s: (0, jnp.minimum(s, pairs - 1)))
+    head = pl.BlockSpec((rows, PAIR), lambda s: (0, jnp.minimum(s, pairs - 1)))
     vm = pltpu.VMEM
     half = block // 2
     torus = (SIDE, SIDE, SIDE, PIECE)
@@ -1017,8 +1034,8 @@
         in_specs=[HBM, head, late(block, d, 1), late(block, g.shape[1], 0), late(half, d, 1), HBM, HBM],
         out_specs=[HBM, WHOLE, WHOLE],
         out_shape=[shape(BF16, rows, d), shape(F32, 2 * pairs, PIECE, HALF), shape(F32, PIECE, 3, 2 * pairs, HALF)],
-        scratch_shapes=[vm((rows, d), BF16), vm(w.shape, BF16), vm(gout.shape, F32), vm((pairs,) + torus + (3 * LANES,), F32), vm((2, block, d), F32), vm((blocks, half, d), F32), vm((2, half, d), BF16),
-                        dma(2, 2, blocks), dma(2, (pairs + 1) * Scatter.SEMS), dma(1, 2), dma(3)] + Scatter.scratch(cut_three(gout.shape[-1])) + Scatter.scratch(cut_three(3 * LANES)) * pairs,
+        scratch_shapes=[vm((rows, d), BF16), vm(w.shape, BF16), vm(gout.shape, F32), vm((pairs,) + torus + (PAIR,), F32), vm((2, block, d), F32), vm((blocks, half, d), F32), vm((2, half, d), BF16),
+                        dma(2, 2, blocks), dma(2, (pairs + 1) * Scatter.SEMS), dma(1, 2), dma(3)] + Scatter.scratch(cut_three(gout.shape[-1])) + Scatter.scratch(cut_three(PAIR)) * pairs,
         compiler_params=params(collective_id),
         name='last',
     )(n1, g, x, g, gh32, w, gout)

time: 268 us -> 267 us (level)
  no operation moved by 1% of the time
where the time goes in v5:
time: 267 us
  Pallas kernels  266 us (100%)
    pallas_call x1, Pallas kernels, back(): pl.pallas_call(functools.partial(back_kernel, pairs), grid=(HEAD_STEP + b...  76.8 us
    pallas_call x1, Pallas kernels, front(): pl.pallas_call(front_kernel, grid=(1 + batch * pairs,), in_specs=[HBM] +...  73.4 us
    pallas_call x1, Pallas kernels, mlp(): pl.pallas_call(functools.partial(mlp_kernel, blocks), grid=(blocks + 1,),...  62.2 us
    pallas_call x1, Pallas kernels, last(): pl.pallas_call(functools.partial(last_kernel, pairs, blocks), grid=(pairs...  47.7 us
    pallas_call x1, Pallas kernels, hand_over(): pl.pallas_call(hand_over_kernel, grid=(rows // block,), in_specs=specs, o...  6.07 us

profile of v5, /device:TPU:1, one launch (start us, length us, event | category | flops | bytes accessed | tf_op | source)
XLA Modules:
  0.0 267.0 jit_solution(3656767810652360848)
XLA Ops:
  0.6 73.4 %front.1 = (bf16[2048,1536]{1,0:T(8,128)(2,1)}, bf16[2048,1536]{1,0:T(8,128)(2,1)}, bf16[2048,512]{1,0:T(8,128)(2,1)}, f32[2,4,2,1024]{3,2,1,0:T(2,128)}, bf16[2...) custom-call(bf16[2048,1024]{1,0:T(8,128)(2,1)} %bitcast.12, ...), custom_call_target="tpu_custom_call" | custom-call | tf_op jit(solution)/shard_map/front/pallas_call | solution.py:655
  74.0 62.2 %mlp.1 = (bf16[2048,1024]{1,0:T(8,128)(2,1)}, bf16[2048,1024]{1,0:T(8,128)(2,1)}, f32[1024,1024]{1,0:T(8,128)}, bf16[2048,4224]{1,0:T(8,128)(2,1)}, bf16[2048,10...) custom-call(bf16[2048,1024]{1,0:T(8,128)(2,1)} %get-tuple-element.34.h_ref, bf16[2048,1024]{1,0:T(8,128)(2,1)} %bitcast.15, ...), custom_call_target="tpu_custom_call" | custom-call | tf_op jit(solution)/shard_map/mlp/pallas_call | solution.py:819
  136.3 76.8 %back.1 = (bf16[2048,1536]{1,0:T(8,128)(2,1)}, f32[1024,512]{1,0:T(8,128)}, f32[16,1408]{1,0:T(8,128)}, f32[16,2,1408]{2,1,0:T(2,128)}) custom-call(f32[4,4,4,16,1408]{4,3,2,1,0:T(8,128)} %get-tuple-element.38.gd_hbm, bf16[2048,1024]{1,0:T(8,128)(2,1)} %get-tuple-element.39.n2_ref, bf16[2048,4224]{1,0:T(8,128)(2,1)} %get-tuple-element.40.act_ref, ...), custom_call_target="tpu_custom_call" | custom-call | tf_op jit(solution)/shard_map/back/pallas_call | solution.py:934
  213.1 47.7 %last.1 = (bf16[2048,1024]{1,0:T(8,128)(2,1)}, f32[8,16,64]{2,1,0:T(8,128)}, f32[16,3,8,64]{3,2,1,0:T(8,128)}) custom-call(bf16[2048,1024]{1,0:T(8,128)(2,1)} %get-tuple-element.37.n1_hbm, bf16[2048,1536]{1,0:T(8,128)(2,1)} %get-tuple-element.47.g_ref.g_row, bf16[2048,1024]{1,0:T(8,128)(2,1)} %bitcast.13, bf16[2048,1536]{1,0:T(8,128)(2,1)} %get-tuple-element.47.g_ref.g_row, ...), custom_call_target="tpu_custom_call" | custom-call | tf_op jit(solution)/shard_map/last/pallas_call | solution.py:1031
  260.8 6.1 %hand_over.1 = (bf16[2048,1024]{1,0:T(8,128)(2,1)}, bf16[2048,1024]{1,0:T(8,128)(2,1)}, f32[16,3,8,64]{3,2,1,0:T(8,128)}, f32[8,16,64]{2,1,0:T(8,128)}, f32[16,2,1408]{2,1,0:T(2,128)}, /*index=5*/f32[16,1408]{1,0:T(8,128)}) custom-call(bf16[2048,1024]{1,0:T(8,128)(2,1)} %get-tuple-element.36.refs_0_, bf16[2048,1024]{1,0:T(8,128)(2,1)} %get-tuple-element.51.refs_1_, ...), custom_call_target="tpu_custom_call" | custom-call | tf_op jit(solution)/shard_map/hand_over/pallas_call | solution.py:1053

commit v6 on v5

--- a/solution.py
+++ b/solution.py
@@ -488,8 +488,8 @@
 CHUNK = 256
 CHUNK_STEPS = 4
 FRONT_PLAN = '014560145260512430,,4,5,1234,,345,,24,,,,3,,,5,,5'
-SCATTER_PLAN = '00,,,,,1,1,,2,0,,,2,12,0,,,,12,0,1,2,012,102,102'
-LAST_PLAN = '00,,11,2,0,1,3,22,3,410,,234,4,201,3,402,1342,01,30241'
+SCATTER_PLAN = '0,0,,,,1,,1,2,02,,,,1,,,2,0,,1,201,2,10,2012,012'
+LAST_PLAN = '00,1,1,,20,13,,2,2,34,10,234,41,,2034,1023,410,2,31402'
 
 
 def to_partner(net, src, dst, send, recv):

time: 267 us -> 268 us (level)
  no operation moved by 1% of the time
where the time goes in v6:
time: 268 us
  Pallas kernels  267 us (100%)
    pallas_call x1, Pallas kernels, back(): pl.pallas_call(functools.partial(back_kernel, pairs), grid=(HEAD_STEP + b...  76.8 us
    pallas_call x1, Pallas kernels, front(): pl.pallas_call(front_kernel, grid=(1 + batch * pairs,), in_specs=[HBM] +...  73.4 us
    pallas_call x1, Pallas kernels, mlp(): pl.pallas_call(functools.partial(mlp_kernel, blocks), grid=(blocks + 1,),...  62.2 us
    pallas_call x1, Pallas kernels, last(): pl.pallas_call(functools.partial(last_kernel, pairs, blocks), grid=(pairs...  48.5 us
    pallas_call x1, Pallas kernels, hand_over(): pl.pallas_call(hand_over_kernel, grid=(rows // block,), in_specs=specs, o...  6.07 us

profile of v6, /device:TPU:1, one launch (start us, length us, event | category | flops | bytes accessed | tf_op | source)
XLA Modules:
  0.0 267.9 jit_solution(15682162917140312191)
XLA Ops:
  0.6 73.4 %front.1 = (bf16[2048,1536]{1,0:T(8,128)(2,1)}, bf16[2048,1536]{1,0:T(8,128)(2,1)}, bf16[2048,512]{1,0:T(8,128)(2,1)}, f32[2,4,2,1024]{3,2,1,0:T(2,128)}, bf16[2...) custom-call(bf16[2048,1024]{1,0:T(8,128)(2,1)} %bitcast.12, ...), custom_call_target="tpu_custom_call" | custom-call | tf_op jit(solution)/shard_map/front/pallas_call | solution.py:655
  74.0 62.2 %mlp.1 = (bf16[2048,1024]{1,0:T(8,128)(2,1)}, bf16[2048,1024]{1,0:T(8,128)(2,1)}, f32[1024,1024]{1,0:T(8,128)}, bf16[2048,4224]{1,0:T(8,128)(2,1)}, bf16[2048,10...) custom-call(bf16[2048,1024]{1,0:T(8,128)(2,1)} %get-tuple-element.34.h_ref, bf16[2048,1024]{1,0:T(8,128)(2,1)} %bitcast.15, ...), custom_call_target="tpu_custom_call" | custom-call | tf_op jit(solution)/shard_map/mlp/pallas_call | solution.py:819
  136.3 76.8 %back.1 = (bf16[2048,1536]{1,0:T(8,128)(2,1)}, f32[1024,512]{1,0:T(8,128)}, f32[16,1408]{1,0:T(8,128)}, f32[16,2,1408]{2,1,0:T(2,128)}) custom-call(f32[4,4,4,16,1408]{4,3,2,1,0:T(8,128)} %get-tuple-element.38.gd_hbm, bf16[2048,1024]{1,0:T(8,128)(2,1)} %get-tuple-element.39.n2_ref, bf16[2048,4224]{1,0:T(8,128)(2,1)} %get-tuple-element.40.act_ref, ...), custom_call_target="tpu_custom_call" | custom-call | tf_op jit(solution)/shard_map/back/pallas_call | solution.py:934
  213.1 48.5 %last.1 = (bf16[2048,1024]{1,0:T(8,128)(2,1)}, f32[8,16,64]{2,1,0:T(8,128)}, f32[16,3,8,64]{3,2,1,0:T(8,128)}) custom-call(bf16[2048,1024]{1,0:T(8,128)(2,1)} %get-tuple-element.37.n1_hbm, bf16[2048,1536]{1,0:T(8,128)(2,1)} %get-tuple-element.47.g_ref.g_row, bf16[2048,1024]{1,0:T(8,128)(2,1)} %bitcast.13, bf16[2048,1536]{1,0:T(8,128)(2,1)} %get-tuple-element.47.g_ref.g_row, ...), custom_call_target="tpu_custom_call" | custom-call | tf_op jit(solution)/shard_map/last/pallas_call | solution.py:1031
  261.6 6.1 %hand_over.1 = (bf16[2048,1024]{1,0:T(8,128)(2,1)}, bf16[2048,1024]{1,0:T(8,128)(2,1)}, f32[16,3,8,64]{3,2,1,0:T(8,128)}, f32[8,16,64]{2,1,0:T(8,128)}, f32[16,2,1408]{2,1,0:T(2,128)}, /*index=5*/f32[16,1408]{1,0:T(8,128)}) custom-call(bf16[2048,1024]{1,0:T(8,128)(2,1)} %get-tuple-element.36.refs_0_, bf16[2048,1024]{1,0:T(8,128)(2,1)} %get-tuple-element.51.refs_1_, ...), custom_call_target="tpu_custom_call" | custom-call | tf_op jit(solution)/shard_map/hand_over/pallas_call | solution.py:1053
